TPU v7x, 32 devices: a 4x4x1 block of a 4x4x8 slice. The times are simulated.
32 devices in a mesh: dp: 1 (over z), hp: 4 (over y), sp: 8 (over x, core).
Axes of the slice: x: 4, y: 4, z: 1, core: 2. Of those that a mesh axis runs over, the one named last changes fastest.
The devices are a block of a 4x4x8 slice.
Arguments:
- tokens: bfloat16 [4, 1024, 2048], P('dp', 'sp')
- theta_q: bfloat16 [2048, 2048], P(None, 'hp')
- theta_k: bfloat16 [2048, 2048], P(None, 'hp')
- theta_v: bfloat16 [2048, 2048], P(None, 'hp')
- w_out: bfloat16 [2048, 2048], P('hp')
- w_one: float32 [16, 128, 512], P('hp')
- b_one: float32 [16, 512], P('hp')
- w_two: float32 [16, 512, 128], P('hp')
- b_two: float32 [16, 128], P('hp')
- ln_gamma: float32 [16, 128], P('hp')
- ln_beta: float32 [16, 128], P('hp')
- inner_lr: float32 [16], P('hp')
Outputs:
- output: bfloat16 [4, 1024, 2048], P('dp', 'sp', 'hp')
All inputs are finite; a program needn't handle non-finite values.
Results may differ from a plain program's by a relative error of at most 0.00195.
Values are sent between devices in bfloat16 or wider.
A program may use at most 768 MiB of HBM per device.

v0:
```python
import jax
import jax.numpy as jnp
from jax import lax
from jax.sharding import PartitionSpec as P

MINI_BATCH = 16
EPS = 1e-6


def inner_apply(params, norm_gain, norm_bias, inputs):
    w_first, b_first, w_second, b_second = params
    hidden = jax.nn.gelu(jnp.dot(inputs, w_first, precision=lax.Precision.HIGHEST) + b_first)
    pre_norm = jnp.dot(hidden, w_second, precision=lax.Precision.HIGHEST) + b_second
    centered = pre_norm - jnp.mean(pre_norm, axis=-1, keepdims=True)
    variance = jnp.mean(centered * centered, axis=-1, keepdims=True)
    return inputs + norm_gain * centered * lax.rsqrt(variance + EPS) + norm_bias


def head_step(params, block, norm_gain, norm_bias, step_size):
    key_blk, value_blk, query_blk = [part_blk.astype(jnp.float32) for part_blk in block]

    def recon_loss(weights):
        residual = inner_apply(weights, norm_gain, norm_bias, key_blk) - value_blk
        return jnp.sum(residual * residual)

    gradients = jax.grad(recon_loss)(params)
    factor = step_size / MINI_BATCH
    updated = tuple(tensor - factor * grad_val for tensor, grad_val in zip(params, gradients))
    return updated, inner_apply(updated, norm_gain, norm_bias, query_blk)


batch_step = jax.vmap(jax.vmap(head_step), in_axes=(0, 0, None, None, None))


def solution(mesh):
    seq_size = mesh.shape["sp"]
    hop_pairs = [(sender, sender + 1) for sender in range(seq_size - 1)]

    def local_fn(tokens, theta_q, theta_k, theta_v, w_out, w_one, b_one, w_two, b_two, ln_gamma, ln_beta, inner_lr):
        batch, tok_dev, model_dim = tokens.shape
        local_heads, head_dim = w_one.shape[0], w_one.shape[1]
        n_blocks = tok_dev // MINI_BATCH
        tok_blocks = tokens.reshape(batch, n_blocks, MINI_BATCH, model_dim)

        def project(weight):
            return jnp.einsum("bnmd,dhe->nbhme", tok_blocks, weight.reshape(model_dim, local_heads, head_dim), preferred_element_type=jnp.float32).astype(jnp.bfloat16)

        blocks = (project(theta_k), project(theta_v), project(theta_q))
        start = tuple(jnp.broadcast_to(tensor, (batch,) + tensor.shape) for tensor in (w_one, b_one, w_two, b_two))
        my_index = lax.axis_index("sp")

        def body(state, block):
            return batch_step(state, block, ln_gamma, ln_beta, inner_lr)

        def run_segment(state, head_out):
            final, produced = lax.scan(body, state, blocks)
            return final, produced.astype(jnp.bfloat16)

        def keep_segment(state, head_out):
            return state, head_out

        def stage(stage_idx, carry):
            return lax.cond(my_index == stage_idx, run_segment, keep_segment, carry[0], carry[1])

        def stage_and_hop(stage_idx, carry):
            state, head_out = stage(stage_idx, carry)
            received = lax.ppermute(state, "sp", hop_pairs)
            take_new = my_index == stage_idx + 1
            state = tuple(jnp.where(take_new, new_val, old_val) for new_val, old_val in zip(received, state))
            return state, head_out

        empty_out = jnp.zeros((n_blocks, batch, local_heads, MINI_BATCH, head_dim), jnp.bfloat16)
        carry = lax.fori_loop(0, seq_size - 1, stage_and_hop, (start, empty_out))
        head_out = stage(seq_size - 1, carry)[1]
        mixed = jnp.einsum("nbhme,hed->bnmd", head_out, w_out.reshape(local_heads, head_dim, model_dim), preferred_element_type=jnp.float32)
        partial_sum = mixed.reshape(batch, tok_dev, model_dim)
        reduced = lax.psum_scatter(partial_sum, "hp", scatter_dimension=2, tiled=True)
        return reduced.astype(jnp.bfloat16)

    head_spec = P("hp", None)
    cube_spec = P("hp", None, None)
    col_spec = P(None, "hp")
    return jax.shard_map(local_fn, mesh=mesh, in_specs=(P("dp", "sp", None), col_spec, col_spec, col_spec, head_spec, cube_spec, head_spec, cube_spec, head_spec, head_spec, head_spec, P("hp")), out_specs=P("dp", "sp", "hp"), check_vma=False)
```

profile of v0, /device:TPU:97, one launch (start us, length us, event | category | flops | bytes accessed | tf_op | source)
XLA Modules:
  0.0 2532.9 jit_solution(11881543412204807501)
XLA Ops:
  6.6 4.1 reshape.142
  10.7 3.5 fusion.90
  14.2 4.1 reshape.144
  18.3 3.5 fusion.87
  23.5 4.0 reshape.145
  27.5 3.5 fusion.84
  31.9 3.8 broadcast_in_dim.62
  39.1 1920.4 %while.64 = (s32[]{:T(128)}, f32[4,4,128,512]{3,2,1,0:T(8,128)}, f32[4,4,512]{2,1,0:T(4,128)S(1)}, f32[4,4,512,128]{3,2,1,0:T(8,128)}, f32[4,4,128]{2,1,0:T(4,12...) while((s32[]{:T(128)}, f32[4,4,128,512]{3,2,1,0:T(8,128)}, ...), condition=%wide.region_13.14_spmd, body=%wide.region_0.13_spmd.sunk | while | flops 1423136768 | bytes 204002240 | solution.py:73
  56.1 4.6 collective-permute-start.2
  62.7 3.7 collective-permute-start.3
  68.3 250.4 %collective-permute-done.3 = f32[4,4,128]{2,1,0:T(4,128)S(1)} collective-permute-done((f32[4,4,128]{2,1,0:T(4,128)S(1)}, f32[4,4,128]{2,1,0:T(4,128)S(1)}, u32[]{:S(2)}, u32[]{:S(2)}) %collective-permute-start.3) | collective-permute-done | bytes 8224 | tf_op jit(solution)/shard_map/while/body/eval_jaxpr/ppermute | solution.py:67
  318.9 4.8 broadcast_select_fusion.10
  323.7 3.3 broadcast_select_fusion.8
  328.9 246.6 %conditional.4 = ((f32[4,4,128,512]{3,2,1,0:T(8,128)}, f32[4,4,512]{2,1,0:T(4,128)S(1)}, f32[4,4,512,128]{3,2,1,0:T(8,128)}, f32[4,4,128]{2,1,0:T(4,128)S(1)}, bf16[8,4,4,16,128]{4,3,2,1,0:T(8,128)(2,1)})) conditional(s32[]{:T(128)} %convert_element_type.117, (f32[4,4,128,512]{3,2,1,0:T(8,128)}, f32[4,4,512]{2,1,0:T(4,128)S(1)}, ...), branch_computations={%region_1.0_spmd, %region_2.12_spmd} | conditional | flops 1421029376 | bytes 111440368 | solution.py:63
  328.9 246.6 %while.62 = (s32[]{:T(128)}, f32[4,4,128,512]{3,2,1,0:T(8,128)}, f32[4,4,512]{2,1,0:T(4,128)S(1)}, f32[4,4,512,128]{3,2,1,0:T(8,128)}, f32[4,4,128]{2,1,0:T(4,12...) while((s32[]{:T(128)}, f32[4,4,128,512]{3,2,1,0:T(8,128)}, ...), condition=%wide.region_12.0_spmd, body=%wide.region_3.10_spmd.sunk | while | flops 1421029376 | bytes 111440208 | solution.py:56
  328.9 3.8 convolution_add_fusion.10
  337.8 3.6 fusion.165
  341.4 3.2 multiply_subtract_fusion.16
  346.3 8.2 multiply_subtract_fusion.18
  359.8 3.8 convolution_add_fusion.10
  368.6 3.6 fusion.165
  377.1 8.2 multiply_subtract_fusion.18
  390.6 3.8 convolution_add_fusion.10
  399.5 3.6 fusion.165
  407.9 8.2 multiply_subtract_fusion.18
  421.4 3.8 convolution_add_fusion.10
  430.3 3.6 fusion.165
  438.8 8.2 multiply_subtract_fusion.18
  452.3 3.8 convolution_add_fusion.10
  461.1 3.6 fusion.165
  469.6 8.2 multiply_subtract_fusion.18
  483.1 3.8 convolution_add_fusion.10
  491.9 3.6 fusion.165
  500.4 8.2 multiply_subtract_fusion.18
  513.9 3.8 convolution_add_fusion.10
  522.8 3.6 fusion.165
  531.2 8.2 multiply_subtract_fusion.18
  544.7 3.8 convolution_add_fusion.10
  553.6 3.6 fusion.165
  562.1 8.2 multiply_subtract_fusion.18
  583.4 84.5 %collective-permute-done.3 = f32[4,4,128]{2,1,0:T(4,128)S(1)} collective-permute-done((f32[4,4,128]{2,1,0:T(4,128)S(1)}, f32[4,4,128]{2,1,0:T(4,128)S(1)}, u32[]{:S(2)}, u32[]{:S(2)}) %collective-permute-start.3) | collective-permute-done | bytes 8224 | tf_op jit(solution)/shard_map/while/body/eval_jaxpr/ppermute | solution.py:67
  668.3 4.8 broadcast_select_fusion.10
  676.2 253.3 %collective-permute-start.2 = (f32[4,4,512,128]{3,2,1,0:T(8,128)}, f32[4,4,512,128]{3,2,1,0:T(8,128)}, u32[]{:S(2)}, u32[]{:S(2)}) collective-permute-start(f32[4,4,512,128]{3,2,1,0:T(8,128)} %get-tuple-element.975), channel_id=1, source_target_pairs={{0,1},{1,2},{2,3},{3,4},{4,5},{5,6},{6,7},{8,9},{9,10},{10,11},{11... | collective-permute-start | bytes 12582920 | tf_op jit(solution)/shard_map/while/body/eval_jaxpr/ppermute | solution.py:67
  935.4 84.5 %collective-permute-done.3 = f32[4,4,128]{2,1,0:T(4,128)S(1)} collective-permute-done((f32[4,4,128]{2,1,0:T(4,128)S(1)}, f32[4,4,128]{2,1,0:T(4,128)S(1)}, u32[]{:S(2)}, u32[]{:S(2)}) %collective-permute-start.3) | collective-permute-done | bytes 8224 | tf_op jit(solution)/shard_map/while/body/eval_jaxpr/ppermute | solution.py:67
  1020.3 4.8 broadcast_select_fusion.10
  1028.2 4.4 collective-permute-start.2
  1032.6 170.7 %collective-permute-start = (f32[4,4,128,512]{3,2,1,0:T(8,128)}, f32[4,4,128,512]{3,2,1,0:T(8,128)}, u32[]{:S(2)}, u32[]{:S(2)}) collective-permute-start(f32[4,4,128,512]{3,2,1,0:T(8,128)} %get-tuple-element.973), channel_id=1, source_target_pairs={{0,1},{1,2},{2,3},{3,4},{4,5},{5,6},{6,7},{8,9},{9,10},{10,11},{11... | collective-permute-start | bytes 12582920 | tf_op jit(solution)/shard_map/while/body/eval_jaxpr/ppermute | solution.py:67
  1207.3 41.6 %collective-permute-done.3 = f32[4,4,128]{2,1,0:T(4,128)S(1)} collective-permute-done((f32[4,4,128]{2,1,0:T(4,128)S(1)}, f32[4,4,128]{2,1,0:T(4,128)S(1)}, u32[]{:S(2)}, u32[]{:S(2)}) %collective-permute-start.3) | collective-permute-done | bytes 8224 | tf_op jit(solution)/shard_map/while/body/eval_jaxpr/ppermute | solution.py:67
  1249.2 4.8 broadcast_select_fusion.10
  1257.1 4.4 collective-permute-start.2
  1261.6 42.4 %collective-permute-start = (f32[4,4,128,512]{3,2,1,0:T(8,128)}, f32[4,4,128,512]{3,2,1,0:T(8,128)}, u32[]{:S(2)}, u32[]{:S(2)}) collective-permute-start(f32[4,4,128,512]{3,2,1,0:T(8,128)} %get-tuple-element.973), channel_id=1, source_target_pairs={{0,1},{1,2},{2,3},{3,4},{4,5},{5,6},{6,7},{8,9},{9,10},{10,11},{11... | collective-permute-start | bytes 12582920 | tf_op jit(solution)/shard_map/while/body/eval_jaxpr/ppermute | solution.py:67
  1304.0 253.3 %collective-permute-start.3 = (f32[4,4,128]{2,1,0:T(4,128)S(1)}, f32[4,4,128]{2,1,0:T(4,128)S(1)}, u32[]{:S(2)}, u32[]{:S(2)}) collective-permute-start(f32[4,4,128]{2,1,0:T(4,128)S(1)} %get-tuple-element.976), channel_id=1, source_target_pairs={{0,1},{1,2},{2,3},{3,4},{4,5},{5,6},{6,7},{8,9},{9,10},{10,11},{11... | collective-permute-start | bytes 24584 | tf_op jit(solution)/shard_map/while/body/eval_jaxpr/ppermute | solution.py:67
  1560.5 4.8 broadcast_select_fusion.10
  1568.4 4.1 collective-permute-start.2
  1572.5 83.5 %collective-permute-start = (f32[4,4,128,512]{3,2,1,0:T(8,128)}, f32[4,4,128,512]{3,2,1,0:T(8,128)}, u32[]{:S(2)}, u32[]{:S(2)}) collective-permute-start(f32[4,4,128,512]{3,2,1,0:T(8,128)} %get-tuple-element.973), channel_id=1, source_target_pairs={{0,1},{1,2},{2,3},{3,4},{4,5},{5,6},{6,7},{8,9},{9,10},{10,11},{11... | collective-permute-start | bytes 12582920 | tf_op jit(solution)/shard_map/while/body/eval_jaxpr/ppermute | solution.py:67
  1656.0 4.4 collective-permute-start.3
  1660.5 170.7 %collective-permute-start.1 = (f32[4,4,512]{2,1,0:T(4,128)S(1)}, f32[4,4,512]{2,1,0:T(4,128)S(1)}, u32[]{:S(2)}, u32[]{:S(2)}) collective-permute-start(f32[4,4,512]{2,1,0:T(4,128)S(1)} %get-tuple-element.974), channel_id=1, source_target_pairs={{0,1},{1,2},{2,3},{3,4},{4,5},{5,6},{6,7},{8,9},{9,10},{10,11},{11... | collective-permute-start | bytes 98312 | tf_op jit(solution)/shard_map/while/body/eval_jaxpr/ppermute | solution.py:67
  1832.2 4.8 broadcast_select_fusion.10
  1840.1 4.3 collective-permute-start.2
  1844.4 40.6 %collective-permute-start = (f32[4,4,128,512]{3,2,1,0:T(8,128)}, f32[4,4,128,512]{3,2,1,0:T(8,128)}, u32[]{:S(2)}, u32[]{:S(2)}) collective-permute-start(f32[4,4,128,512]{3,2,1,0:T(8,128)} %get-tuple-element.973), channel_id=1, source_target_pairs={{0,1},{1,2},{2,3},{3,4},{4,5},{5,6},{6,7},{8,9},{9,10},{10,11},{11... | collective-permute-start | bytes 12582920 | tf_op jit(solution)/shard_map/while/body/eval_jaxpr/ppermute | solution.py:67
  1885.0 4.4 collective-permute-start.3
  1889.4 42.4 %collective-permute-start.1 = (f32[4,4,512]{2,1,0:T(4,128)S(1)}, f32[4,4,512]{2,1,0:T(4,128)S(1)}, u32[]{:S(2)}, u32[]{:S(2)}) collective-permute-start(f32[4,4,512]{2,1,0:T(4,128)S(1)} %get-tuple-element.974), channel_id=1, source_target_pairs={{0,1},{1,2},{2,3},{3,4},{4,5},{5,6},{6,7},{8,9},{9,10},{10,11},{11... | collective-permute-start | bytes 98312 | tf_op jit(solution)/shard_map/while/body/eval_jaxpr/ppermute | solution.py:67
  1935.2 4.8 broadcast_select_fusion.10
  1964.1 559.7 %reduce-scatter.2.cloned.1.call-done = f32[4,128,512]{2,1,0:T(8,128)} async-done(((f32[4,128,2048]{2,1,0:T(8,128)}), f32[4,128,512]{2,1,0:T(8,128)}) %reduce-scatter.2.cloned.1.call-update) | async-done | bytes 1048592 | tf_op jit(solution)/shard_map/reduce_scatter | solution.py:77
  (339 shorter events, 180.4 us)
Async XLA Ops:
  6.5 1952.9 %copy-start = (bf16[512,2048]{1,0:T(8,128)(2,1)S(1)}, bf16[512,2048]{1,0:T(8,128)(2,1)}, u32[]{:S(2)}) copy-start(bf16[512,2048]{1,0:T(8,128)(2,1)} %param.26) | copy-start | bytes 6291460
  6.6 2517.2 %reduce-scatter.2.cloned.1.call-start = ((), (), s32[]{:S(2)}) async-start(), calls=%async_computation.1 | async-start | bytes 5242880 | tf_op jit(solution)/shard_map/reduce_scatter | solution.py:77
  14.2 7.7 copy-start.13
  31.8 3.9 copy-start.16
  31.9 6.2 copy-start.17
  31.9 6.2 copy-start.18
  56.1 262.7 %collective-permute-start.2 = (f32[4,4,512,128]{3,2,1,0:T(8,128)}, f32[4,4,512,128]{3,2,1,0:T(8,128)}, u32[]{:S(2)}, u32[]{:S(2)}) collective-permute-start(f32[4,4,512,128]{3,2,1,0:T(8,128)} %get-tuple-element.975), channel_id=1, source_target_pairs={{0,1},{1,2},{2,3},{3,4},{4,5},{5,6},{6,7},{8,9},{9,10},{10,11},{11... | collective-permute-start | bytes 12582920 | tf_op jit(solution)/shard_map/while/body/eval_jaxpr/ppermute | solution.py:67
  60.7 263.0 %collective-permute-start = (f32[4,4,128,512]{3,2,1,0:T(8,128)}, f32[4,4,128,512]{3,2,1,0:T(8,128)}, u32[]{:S(2)}, u32[]{:S(2)}) collective-permute-start(f32[4,4,128,512]{3,2,1,0:T(8,128)} %get-tuple-element.973), channel_id=1, source_target_pairs={{0,1},{1,2},{2,3},{3,4},{4,5},{5,6},{6,7},{8,9},{9,10},{10,11},{11... | collective-permute-start | bytes 12582920 | tf_op jit(solution)/shard_map/while/body/eval_jaxpr/ppermute | solution.py:67
  62.7 256.1 %collective-permute-start.3 = (f32[4,4,128]{2,1,0:T(4,128)S(1)}, f32[4,4,128]{2,1,0:T(4,128)S(1)}, u32[]{:S(2)}, u32[]{:S(2)}) collective-permute-start(f32[4,4,128]{2,1,0:T(4,128)S(1)} %get-tuple-element.976), channel_id=1, source_target_pairs={{0,1},{1,2},{2,3},{3,4},{4,5},{5,6},{6,7},{8,9},{9,10},{10,11},{11... | collective-permute-start | bytes 24584 | tf_op jit(solution)/shard_map/while/body/eval_jaxpr/ppermute | solution.py:67
  66.4 252.5 %collective-permute-start.1 = (f32[4,4,512]{2,1,0:T(4,128)S(1)}, f32[4,4,512]{2,1,0:T(4,128)S(1)}, u32[]{:S(2)}, u32[]{:S(2)}) collective-permute-start(f32[4,4,512]{2,1,0:T(4,128)S(1)} %get-tuple-element.974), channel_id=1, source_target_pairs={{0,1},{1,2},{2,3},{3,4},{4,5},{5,6},{6,7},{8,9},{9,10},{10,11},{11... | collective-permute-start | bytes 98312 | tf_op jit(solution)/shard_map/while/body/eval_jaxpr/ppermute | solution.py:67
  318.8 4.8 copy-start.7
  328.9 3.8 copy-start.1
  335.1 6.3 copy-start.5
  344.6 14.1 copy-start.6
  359.8 3.8 copy-start.1
  366.0 6.3 copy-start.5
  375.4 14.1 copy-start.6
  390.6 3.8 copy-start.1
  396.8 6.3 copy-start.5
  406.3 14.1 copy-start.6
  421.4 3.8 copy-start.1
  427.6 6.3 copy-start.5
  437.1 14.1 copy-start.6
  452.3 3.8 copy-start.1
  458.5 6.3 copy-start.5
  467.9 14.1 copy-start.6
  483.1 3.8 copy-start.1
  489.3 6.3 copy-start.5
  498.7 14.1 copy-start.6
  513.9 3.8 copy-start.1
  520.1 6.3 copy-start.5
  529.6 14.1 copy-start.6
  550.9 6.3 copy-start.5
  560.4 14.1 copy-start.6
  575.6 92.8 %collective-permute-start.2 = (f32[4,4,512,128]{3,2,1,0:T(8,128)}, f32[4,4,512,128]{3,2,1,0:T(8,128)}, u32[]{:S(2)}, u32[]{:S(2)}) collective-permute-start(f32[4,4,512,128]{3,2,1,0:T(8,128)} %get-tuple-element.975), channel_id=1, source_target_pairs={{0,1},{1,2},{2,3},{3,4},{4,5},{5,6},{6,7},{8,9},{9,10},{10,11},{11... | collective-permute-start | bytes 12582920 | tf_op jit(solution)/shard_map/while/body/eval_jaxpr/ppermute | solution.py:67
  577.5 95.6 %collective-permute-start = (f32[4,4,128,512]{3,2,1,0:T(8,128)}, f32[4,4,128,512]{3,2,1,0:T(8,128)}, u32[]{:S(2)}, u32[]{:S(2)}) collective-permute-start(f32[4,4,128,512]{3,2,1,0:T(8,128)} %get-tuple-element.973), channel_id=1, source_target_pairs={{0,1},{1,2},{2,3},{3,4},{4,5},{5,6},{6,7},{8,9},{9,10},{10,11},{11... | collective-permute-start | bytes 12582920 | tf_op jit(solution)/shard_map/while/body/eval_jaxpr/ppermute | solution.py:67
  579.5 88.5 %collective-permute-start.3 = (f32[4,4,128]{2,1,0:T(4,128)S(1)}, f32[4,4,128]{2,1,0:T(4,128)S(1)}, u32[]{:S(2)}, u32[]{:S(2)}) collective-permute-start(f32[4,4,128]{2,1,0:T(4,128)S(1)} %get-tuple-element.976), channel_id=1, source_target_pairs={{0,1},{1,2},{2,3},{3,4},{4,5},{5,6},{6,7},{8,9},{9,10},{10,11},{11... | collective-permute-start | bytes 24584 | tf_op jit(solution)/shard_map/while/body/eval_jaxpr/ppermute | solution.py:67
  581.4 86.9 %collective-permute-start.1 = (f32[4,4,512]{2,1,0:T(4,128)S(1)}, f32[4,4,512]{2,1,0:T(4,128)S(1)}, u32[]{:S(2)}, u32[]{:S(2)}) collective-permute-start(f32[4,4,512]{2,1,0:T(4,128)S(1)} %get-tuple-element.974), channel_id=1, source_target_pairs={{0,1},{1,2},{2,3},{3,4},{4,5},{5,6},{6,7},{8,9},{9,10},{10,11},{11... | collective-permute-start | bytes 98312 | tf_op jit(solution)/shard_map/while/body/eval_jaxpr/ppermute | solution.py:67
  668.3 4.8 copy-start.7
  676.2 344.1 %collective-permute-start.2 = (f32[4,4,512,128]{3,2,1,0:T(8,128)}, f32[4,4,512,128]{3,2,1,0:T(8,128)}, u32[]{:S(2)}, u32[]{:S(2)}) collective-permute-start(f32[4,4,512,128]{3,2,1,0:T(8,128)} %get-tuple-element.975), channel_id=1, source_target_pairs={{0,1},{1,2},{2,3},{3,4},{4,5},{5,6},{6,7},{8,9},{9,10},{10,11},{11... | collective-permute-start | bytes 12582920 | tf_op jit(solution)/shard_map/while/body/eval_jaxpr/ppermute | solution.py:67
  929.5 95.6 %collective-permute-start = (f32[4,4,128,512]{3,2,1,0:T(8,128)}, f32[4,4,128,512]{3,2,1,0:T(8,128)}, u32[]{:S(2)}, u32[]{:S(2)}) collective-permute-start(f32[4,4,128,512]{3,2,1,0:T(8,128)} %get-tuple-element.973), channel_id=1, source_target_pairs={{0,1},{1,2},{2,3},{3,4},{4,5},{5,6},{6,7},{8,9},{9,10},{10,11},{11... | collective-permute-start | bytes 12582920 | tf_op jit(solution)/shard_map/while/body/eval_jaxpr/ppermute | solution.py:67
  931.5 88.5 %collective-permute-start.3 = (f32[4,4,128]{2,1,0:T(4,128)S(1)}, f32[4,4,128]{2,1,0:T(4,128)S(1)}, u32[]{:S(2)}, u32[]{:S(2)}) collective-permute-start(f32[4,4,128]{2,1,0:T(4,128)S(1)} %get-tuple-element.976), channel_id=1, source_target_pairs={{0,1},{1,2},{2,3},{3,4},{4,5},{5,6},{6,7},{8,9},{9,10},{10,11},{11... | collective-permute-start | bytes 24584 | tf_op jit(solution)/shard_map/while/body/eval_jaxpr/ppermute | solution.py:67
  933.4 86.9 %collective-permute-start.1 = (f32[4,4,512]{2,1,0:T(4,128)S(1)}, f32[4,4,512]{2,1,0:T(4,128)S(1)}, u32[]{:S(2)}, u32[]{:S(2)}) collective-permute-start(f32[4,4,512]{2,1,0:T(4,128)S(1)} %get-tuple-element.974), channel_id=1, source_target_pairs={{0,1},{1,2},{2,3},{3,4},{4,5},{5,6},{6,7},{8,9},{9,10},{10,11},{11... | collective-permute-start | bytes 98312 | tf_op jit(solution)/shard_map/while/body/eval_jaxpr/ppermute | solution.py:67
  1020.3 4.8 copy-start.7
  1028.2 221.0 %collective-permute-start.2 = (f32[4,4,512,128]{3,2,1,0:T(8,128)}, f32[4,4,512,128]{3,2,1,0:T(8,128)}, u32[]{:S(2)}, u32[]{:S(2)}) collective-permute-start(f32[4,4,512,128]{3,2,1,0:T(8,128)} %get-tuple-element.975), channel_id=1, source_target_pairs={{0,1},{1,2},{2,3},{3,4},{4,5},{5,6},{6,7},{8,9},{9,10},{10,11},{11... | collective-permute-start | bytes 12582920 | tf_op jit(solution)/shard_map/while/body/eval_jaxpr/ppermute | solution.py:67
  1032.6 221.4 %collective-permute-start = (f32[4,4,128,512]{3,2,1,0:T(8,128)}, f32[4,4,128,512]{3,2,1,0:T(8,128)}, u32[]{:S(2)}, u32[]{:S(2)}) collective-permute-start(f32[4,4,128,512]{3,2,1,0:T(8,128)} %get-tuple-element.973), channel_id=1, source_target_pairs={{0,1},{1,2},{2,3},{3,4},{4,5},{5,6},{6,7},{8,9},{9,10},{10,11},{11... | collective-permute-start | bytes 12582920 | tf_op jit(solution)/shard_map/while/body/eval_jaxpr/ppermute | solution.py:67
  1203.4 45.5 %collective-permute-start.3 = (f32[4,4,128]{2,1,0:T(4,128)S(1)}, f32[4,4,128]{2,1,0:T(4,128)S(1)}, u32[]{:S(2)}, u32[]{:S(2)}) collective-permute-start(f32[4,4,128]{2,1,0:T(4,128)S(1)} %get-tuple-element.976), channel_id=1, source_target_pairs={{0,1},{1,2},{2,3},{3,4},{4,5},{5,6},{6,7},{8,9},{9,10},{10,11},{11... | collective-permute-start | bytes 24584 | tf_op jit(solution)/shard_map/while/body/eval_jaxpr/ppermute | solution.py:67
  1205.3 43.9 %collective-permute-start.1 = (f32[4,4,512]{2,1,0:T(4,128)S(1)}, f32[4,4,512]{2,1,0:T(4,128)S(1)}, u32[]{:S(2)}, u32[]{:S(2)}) collective-permute-start(f32[4,4,512]{2,1,0:T(4,128)S(1)} %get-tuple-element.974), channel_id=1, source_target_pairs={{0,1},{1,2},{2,3},{3,4},{4,5},{5,6},{6,7},{8,9},{9,10},{10,11},{11... | collective-permute-start | bytes 98312 | tf_op jit(solution)/shard_map/while/body/eval_jaxpr/ppermute | solution.py:67
  1249.2 4.8 copy-start.7
  1257.1 303.3 %collective-permute-start.2 = (f32[4,4,512,128]{3,2,1,0:T(8,128)}, f32[4,4,512,128]{3,2,1,0:T(8,128)}, u32[]{:S(2)}, u32[]{:S(2)}) collective-permute-start(f32[4,4,512,128]{3,2,1,0:T(8,128)} %get-tuple-element.975), channel_id=1, source_target_pairs={{0,1},{1,2},{2,3},{3,4},{4,5},{5,6},{6,7},{8,9},{9,10},{10,11},{11... | collective-permute-start | bytes 12582920 | tf_op jit(solution)/shard_map/while/body/eval_jaxpr/ppermute | solution.py:67
  1261.6 303.7 %collective-permute-start = (f32[4,4,128,512]{3,2,1,0:T(8,128)}, f32[4,4,128,512]{3,2,1,0:T(8,128)}, u32[]{:S(2)}, u32[]{:S(2)}) collective-permute-start(f32[4,4,128,512]{3,2,1,0:T(8,128)} %get-tuple-element.973), channel_id=1, source_target_pairs={{0,1},{1,2},{2,3},{3,4},{4,5},{5,6},{6,7},{8,9},{9,10},{10,11},{11... | collective-permute-start | bytes 12582920 | tf_op jit(solution)/shard_map/while/body/eval_jaxpr/ppermute | solution.py:67
  1304.0 255.3 %collective-permute-start.3 = (f32[4,4,128]{2,1,0:T(4,128)S(1)}, f32[4,4,128]{2,1,0:T(4,128)S(1)}, u32[]{:S(2)}, u32[]{:S(2)}) collective-permute-start(f32[4,4,128]{2,1,0:T(4,128)S(1)} %get-tuple-element.976), channel_id=1, source_target_pairs={{0,1},{1,2},{2,3},{3,4},{4,5},{5,6},{6,7},{8,9},{9,10},{10,11},{11... | collective-permute-start | bytes 24584 | tf_op jit(solution)/shard_map/while/body/eval_jaxpr/ppermute | solution.py:67
  1557.3 3.1 collective-permute-start.1
  1560.5 4.8 copy-start.7
  1568.4 263.8 %collective-permute-start.2 = (f32[4,4,512,128]{3,2,1,0:T(8,128)}, f32[4,4,512,128]{3,2,1,0:T(8,128)}, u32[]{:S(2)}, u32[]{:S(2)}) collective-permute-start(f32[4,4,512,128]{3,2,1,0:T(8,128)} %get-tuple-element.975), channel_id=1, source_target_pairs={{0,1},{1,2},{2,3},{3,4},{4,5},{5,6},{6,7},{8,9},{9,10},{10,11},{11... | collective-permute-start | bytes 12582920 | tf_op jit(solution)/shard_map/while/body/eval_jaxpr/ppermute | solution.py:67
  1572.5 264.6 %collective-permute-start = (f32[4,4,128,512]{3,2,1,0:T(8,128)}, f32[4,4,128,512]{3,2,1,0:T(8,128)}, u32[]{:S(2)}, u32[]{:S(2)}) collective-permute-start(f32[4,4,128,512]{3,2,1,0:T(8,128)} %get-tuple-element.973), channel_id=1, source_target_pairs={{0,1},{1,2},{2,3},{3,4},{4,5},{5,6},{6,7},{8,9},{9,10},{10,11},{11... | collective-permute-start | bytes 12582920 | tf_op jit(solution)/shard_map/while/body/eval_jaxpr/ppermute | solution.py:67
  1656.0 175.2 %collective-permute-start.3 = (f32[4,4,128]{2,1,0:T(4,128)S(1)}, f32[4,4,128]{2,1,0:T(4,128)S(1)}, u32[]{:S(2)}, u32[]{:S(2)}) collective-permute-start(f32[4,4,128]{2,1,0:T(4,128)S(1)} %get-tuple-element.976), channel_id=1, source_target_pairs={{0,1},{1,2},{2,3},{3,4},{4,5},{5,6},{6,7},{8,9},{9,10},{10,11},{11... | collective-permute-start | bytes 24584 | tf_op jit(solution)/shard_map/while/body/eval_jaxpr/ppermute | solution.py:67
  1660.5 171.7 %collective-permute-start.1 = (f32[4,4,512]{2,1,0:T(4,128)S(1)}, f32[4,4,512]{2,1,0:T(4,128)S(1)}, u32[]{:S(2)}, u32[]{:S(2)}) collective-permute-start(f32[4,4,512]{2,1,0:T(4,128)S(1)} %get-tuple-element.974), channel_id=1, source_target_pairs={{0,1},{1,2},{2,3},{3,4},{4,5},{5,6},{6,7},{8,9},{9,10},{10,11},{11... | collective-permute-start | bytes 98312 | tf_op jit(solution)/shard_map/while/body/eval_jaxpr/ppermute | solution.py:67
  1832.2 4.8 copy-start.7
  1840.1 95.1 %collective-permute-start.2 = (f32[4,4,512,128]{3,2,1,0:T(8,128)}, f32[4,4,512,128]{3,2,1,0:T(8,128)}, u32[]{:S(2)}, u32[]{:S(2)}) collective-permute-start(f32[4,4,512,128]{3,2,1,0:T(8,128)} %get-tuple-element.975), channel_id=1, source_target_pairs={{0,1},{1,2},{2,3},{3,4},{4,5},{5,6},{6,7},{8,9},{9,10},{10,11},{11... | collective-permute-start | bytes 12582920 | tf_op jit(solution)/shard_map/while/body/eval_jaxpr/ppermute | solution.py:67
  1844.4 95.6 %collective-permute-start = (f32[4,4,128,512]{3,2,1,0:T(8,128)}, f32[4,4,128,512]{3,2,1,0:T(8,128)}, u32[]{:S(2)}, u32[]{:S(2)}) collective-permute-start(f32[4,4,128,512]{3,2,1,0:T(8,128)} %get-tuple-element.973), channel_id=1, source_target_pairs={{0,1},{1,2},{2,3},{3,4},{4,5},{5,6},{6,7},{8,9},{9,10},{10,11},{11... | collective-permute-start | bytes 12582920 | tf_op jit(solution)/shard_map/while/body/eval_jaxpr/ppermute | solution.py:67
  1885.0 49.9 %collective-permute-start.3 = (f32[4,4,128]{2,1,0:T(4,128)S(1)}, f32[4,4,128]{2,1,0:T(4,128)S(1)}, u32[]{:S(2)}, u32[]{:S(2)}) collective-permute-start(f32[4,4,128]{2,1,0:T(4,128)S(1)} %get-tuple-element.976), channel_id=1, source_target_pairs={{0,1},{1,2},{2,3},{3,4},{4,5},{5,6},{6,7},{8,9},{9,10},{10,11},{11... | collective-permute-start | bytes 24584 | tf_op jit(solution)/shard_map/while/body/eval_jaxpr/ppermute | solution.py:67
  1889.4 45.8 %collective-permute-start.1 = (f32[4,4,512]{2,1,0:T(4,128)S(1)}, f32[4,4,512]{2,1,0:T(4,128)S(1)}, u32[]{:S(2)}, u32[]{:S(2)}) collective-permute-start(f32[4,4,512]{2,1,0:T(4,128)S(1)} %get-tuple-element.974), channel_id=1, source_target_pairs={{0,1},{1,2},{2,3},{3,4},{4,5},{5,6},{6,7},{8,9},{9,10},{10,11},{11... | collective-permute-start | bytes 98312 | tf_op jit(solution)/shard_map/while/body/eval_jaxpr/ppermute | solution.py:67
  1935.2 4.8 copy-start.7
  (21 other events, 44.9 us)
Sparse Core Ops, SparseCore 0:
  1964.2 559.5 reduce-scatter.1
where the time goes:
time: 2540 us; the launch traced here: 2530 us
  starting transfers between devices  1110 us (44%)
  waiting for transfers between devices  1030 us (41%)
  matrix products  213 us (8%)
  other arithmetic  76.9 us (3%)
  local copies, waits for them, and re-layouts  52.1 us (2%)
  loops' own time  35 us (1%)
    ppermute x28, starting transfers between devices, stage_and_hop(): received = lax.ppermute(state, 'sp', hop_pairs)  1110 us
    reduce_scatter x1, waiting for transfers between devices, local_fn(): lax.psum_scatter(partial_sum, 'hp', scatter_dimension=2, tiled=True)  560 us
    ppermute x28, waiting for transfers between devices, stage_and_hop(): received = lax.ppermute(state, 'sp', hop_pairs)  468 us
    dot_general x32, matrix products, inner_apply(): jnp.dot(hidden, w_second, precision=lax.Precision.HIGHEST) + b_second  132 us
    dot_general x24, matrix products, inner_apply(): jnp.dot(inputs, w_first, precision=lax.Precision.HIGHEST) + b_first  68.4 us
  transfers between devices with their start and end apart: 29, of which 12 were waited for; matrix products, arithmetic and copies ran while one was open for 1% of the time, Pallas kernels for 0%

commit v1 on v0

v1 whole, which is shorter than its diff:
```python
import functools

import jax
import jax.numpy as jnp
from jax import lax
from jax.experimental import pallas as pl
from jax.experimental.pallas import tpu as pltpu
from jax.sharding import PartitionSpec as P

MINI = 16
EPS = 1e-6
GELU_A = 0.7978845608028654
GELU_B = 0.044715
F32 = jnp.float32
BF16 = jnp.bfloat16


def split3(x):
    high = x.astype(BF16)
    rest = x - high.astype(F32)
    mid = rest.astype(BF16)
    low = (rest - mid.astype(F32)).astype(BF16)
    return high, mid, low


def dot(a, b):
    return jnp.dot(a, b, preferred_element_type=F32)


def dot_t(a, b):
    return lax.dot_general(a, b, (((1,), (1,)), ((), ())), preferred_element_type=F32)


def six(parts):
    high, mid, low = parts
    return [high, mid, low, high, mid, high]


def six_other(parts):
    high, mid, low = parts
    return [high, high, high, mid, mid, low]


def ttt_kernel(n_chains, kvq, w1, b1, w2, b2, gamma, beta, rate, out, *scr):
    n_blocks, block = kvq.shape[0], kvq.shape[3]
    per_block = block // MINI
    n_steps = n_blocks * per_block
    dim, hid = w1.shape
    per = len(scr) // n_chains
    chains = [scr[i * per:(i + 1) * per] for i in range(n_chains)]
    factor = rate[0, 0] / MINI
    gain, bias = gamma[...], beta[...]

    def load(chain, which, step):
        return kvq[step // per_block, chain, which, pl.ds(pl.multiple_of((step % per_block) * MINI, MINI), MINI), :]

    def store_first(refs, value):
        w1f, w1hm, w1lo = refs
        high, mid, low = split3(value)
        w1f[...] = value
        w1hm[:dim] = high
        w1hm[dim:] = mid
        w1lo[...] = low

    def correction(x, keys):
        rep = jnp.concatenate([keys] * 8, axis=0)
        a = dot_t(x, rep) + 1.0
        high, mid, low = split3(a)
        lane = lax.broadcasted_iota(jnp.int32, a.shape, 1)
        part = jnp.where(lane < 3 * MINI, high.astype(F32), jnp.where(lane < 5 * MINI, mid.astype(F32), low.astype(F32)))
        return jnp.where(lane < 6 * MINI, part, 0.0).astype(BF16)

    def base(x, w1hm, w1lo, b1r):
        return dot(jnp.concatenate([x, x], axis=1), w1hm[...]) + dot(x, w1lo[...]) + b1r[...]

    zeros32 = jnp.zeros((2 * MINI, hid), BF16)

    for c in range(n_chains):
        w1f, w1hm, w1lo, w2f, w2hm, w2lo, b1r, b2r, zb, cor, dh8 = chains[c]
        store_first((w1f, w1hm, w1lo), w1[...])
        w2t = w2[...].T
        w2t = w2t - jnp.mean(w2t, axis=0, keepdims=True)
        store_first((w2f, w2hm, w2lo), w2t)
        b1r[...] = b1[...]
        b2r[...] = b2[...] - jnp.mean(b2[...], axis=1, keepdims=True)
        dh8[...] = jnp.zeros_like(dh8)
        cor[...] = jnp.zeros_like(cor)
        zb[...] = base(jnp.concatenate([load(c, 2, 0), load(c, 0, 0)], axis=0), w1hm, w1lo, b1r)

    def step_chain(c, step):
        w1f, w1hm, w1lo, w2f, w2hm, w2lo, b1r, b2r, zb, cor, dh8 = chains[c]
        after = jnp.minimum(step + 1, n_steps - 1)
        before = jnp.maximum(step - 1, 0)
        key, val, qry = load(c, 0, step), load(c, 1, step), load(c, 2, step)
        key_before, qry_before = load(c, 0, before), load(c, 2, before)
        key_f, val_f, qry_f = key.astype(F32), val.astype(F32), qry_before.astype(F32)

        z = zb[...] - dot(cor[...], dh8[...])
        yield

        keys_t = jnp.concatenate([key_before] * 3 + [jnp.zeros((5 * MINI, dim), BF16)], axis=0).T
        new_w1 = w1f[...] - dot(keys_t, dh8[...])
        store_first((w1f, w1hm, w1lo), new_w1)
        yield

        z2 = z * z
        t = jnp.tanh(z * (GELU_A + (GELU_A * GELU_B) * z2))
        cdf = 0.5 + 0.5 * t
        h = z * cdf
        zk, z2k, tk = z[MINI:], z2[MINI:], t[MINI:]
        slope = cdf[MINI:] + (0.5 * zk * (1.0 - tk * tk)) * (GELU_A + (3.0 * GELU_A * GELU_B) * z2k)
        hp = split3(h)
        r = dot_t(jnp.concatenate(hp, axis=0), w2hm[...])
        yl = dot_t(hp[0], w2lo[...])
        yield

        x_after = jnp.concatenate([qry, load(c, 0, after)], axis=0)
        zb[...] = base(x_after, w1hm, w1lo, b1r)
        cor[...] = correction(x_after, key)
        yield

        n2 = 2 * MINI
        r = r[:, :dim] + r[:, dim:]
        yc = r[:n2] + r[n2:2 * n2] + r[2 * n2:] + yl + b2r[...]
        var = jnp.mean(yc * yc, axis=1, keepdims=True)
        rstd = lax.rsqrt(var + EPS)
        xhat = yc * rstd
        out[before // per_block, c, pl.ds(pl.multiple_of((before % per_block) * MINI, MINI), MINI), :] = (
            qry_f + gain * xhat[:MINI] + bias).astype(BF16)

        xk = xhat[MINI:]
        dx = (key_f + gain * xk + bias - val_f) * ((2.0 * factor) * gain)
        m1 = jnp.mean(dx, axis=1, keepdims=True)
        m2 = jnp.mean(dx * xk, axis=1, keepdims=True)
        dy = rstd[MINI:] * (dx - m1 - xk * m2)
        dyp = split3(dy)
        d3 = jnp.concatenate(dyp, axis=0)
        e = dot(jnp.concatenate([d3, d3], axis=1), w2hm[...])
        el = dot(dyp[0], w2lo[...])
        yield

        hk8 = jnp.concatenate(six([p[MINI:] for p in hp]) + [zeros32], axis=0)
        dy_t = jnp.concatenate(six_other(dyp) + [jnp.zeros((2 * MINI, dim), BF16)], axis=0).T
        new_w2 = w2f[...] - dot(dy_t, hk8)
        store_first((w2f, w2hm, w2lo), new_w2)
        b2r[...] = b2r[...] - jnp.sum(dy, axis=0, keepdims=True)
        yield

        dh = (e[:MINI] + e[MINI:2 * MINI] + e[2 * MINI:] + el) * slope
        dhp = six(split3(dh))
        dh8[:6 * MINI] = jnp.concatenate(dhp, axis=0)
        b1r[...] = b1r[...] - jnp.sum(dh, axis=0, keepdims=True)

    def body(step, carry):
        running = [step_chain(c, step) for c in range(n_chains)]
        while running:
            running = [g for g in running if next(g, 1) is None]
        return carry

    lax.fori_loop(0, n_steps, body, 0)

    for c in range(n_chains):
        w1f, w1hm, w1lo, w2f, w2hm, w2lo, b1r, b2r, zb, cor, dh8 = chains[c]
        qry = load(c, 2, n_steps - 1)
        z = zb[:MINI] - dot(cor[...], dh8[...])[:MINI]
        t = jnp.tanh(z * (GELU_A + (GELU_A * GELU_B) * (z * z)))
        h = z * (0.5 + 0.5 * t)
        hp = split3(h)
        r = dot_t(jnp.concatenate(hp, axis=0), w2hm[...])
        r = r[:, :dim] + r[:, dim:]
        yc = r[:MINI] + r[MINI:2 * MINI] + r[2 * MINI:] + dot_t(hp[0], w2lo[...]) + b2r[...]
        xhat = yc * lax.rsqrt(jnp.mean(yc * yc, axis=1, keepdims=True) + EPS)
        out[n_blocks - 1, c, pl.ds(block - MINI, MINI), :] = (qry.astype(F32) + gain * xhat + bias).astype(BF16)


def run_chains(kvq, w1, b1, w2, b2, gamma, beta, rate):
    n_blocks, n_chains, _, block, dim = kvq.shape
    hid = w1.shape[1]
    vmem = pl.BlockSpec(memory_space=pltpu.VMEM)
    per_chain = [
        pltpu.VMEM((dim, hid), F32), pltpu.VMEM((2 * dim, hid), BF16), pltpu.VMEM((dim, hid), BF16),
        pltpu.VMEM((dim, hid), F32), pltpu.VMEM((2 * dim, hid), BF16), pltpu.VMEM((dim, hid), BF16),
        pltpu.VMEM((1, hid), F32), pltpu.VMEM((1, dim), F32), pltpu.VMEM((2 * MINI, hid), F32),
        pltpu.VMEM((2 * MINI, 8 * MINI), BF16), pltpu.VMEM((8 * MINI, hid), BF16),
    ]
    return pl.pallas_call(
        functools.partial(ttt_kernel, n_chains),
        out_shape=jax.ShapeDtypeStruct((n_blocks, n_chains, block, dim), BF16),
        in_specs=[vmem] * 7 + [pl.BlockSpec(memory_space=pltpu.SMEM)],
        out_specs=vmem,
        scratch_shapes=per_chain * n_chains,
    )(kvq, w1, b1, w2, b2, gamma, beta, rate)


def solution(mesh):
    sp = mesh.shape["sp"]
    hp = mesh.shape["hp"]

    def local_fn(tokens, theta_q, theta_k, theta_v, w_out, w_one, b_one, w_two, b_two, ln_gamma, ln_beta, inner_lr):
        batch, block, model = tokens.shape
        heads, dim = w_one.shape[0], w_one.shape[1]
        n_chains = heads * batch // sp
        flat = tokens.reshape(batch * block, model)

        def project(theta):
            p = jnp.dot(flat, theta, preferred_element_type=F32).astype(BF16)
            p = p.reshape(batch, block, heads, dim).transpose(2, 0, 1, 3)
            return p.reshape(sp, n_chains, 1, block, dim)

        kvq = jnp.concatenate([project(theta_k), project(theta_v), project(theta_q)], axis=2)
        kvq = lax.all_to_all(kvq, "sp", 0, 0, tiled=True)

        first = lax.axis_index("sp") * n_chains
        head = first // batch

        def pick(arr):
            return lax.dynamic_index_in_dim(arr, head, 0, keepdims=False)

        got = run_chains(kvq, pick(w_one), pick(b_one)[None], pick(w_two), pick(b_two)[None], pick(ln_gamma)[None],
                         pick(ln_beta)[None], pick(inner_lr).reshape(1, 1))
        got = lax.all_to_all(got, "sp", 0, 0, tiled=True)
        got = got.reshape(heads, batch, block, dim)
        got = lax.all_gather(got, "hp", axis=0, tiled=True)
        w_cols = lax.all_to_all(w_out, "hp", 1, 0, tiled=True)
        rows = got.transpose(1, 2, 0, 3).reshape(batch * block, hp * heads * dim)
        res = jnp.dot(rows, w_cols, preferred_element_type=F32).astype(BF16)
        return res.reshape(batch, block, model // hp)

    head_spec = P("hp", None)
    cube_spec = P("hp", None, None)
    col_spec = P(None, "hp")
    return jax.shard_map(local_fn, mesh=mesh, in_specs=(P("dp", "sp", None), col_spec, col_spec, col_spec, head_spec, cube_spec, head_spec, cube_spec, head_spec, head_spec, head_spec, P("hp")), out_specs=P("dp", "sp", "hp"), check_vma=False)
```

time: 2540 us -> 203 us (0.08)
  starting transfers between devices: 1110 us -> 6.34 us
  waiting for transfers between devices: 1030 us -> 12.9 us
  matrix products: 213 us -> 12.2 us
  other arithmetic: 76.9 us -> 2.37 us
  Pallas kernels: 0 us -> 68.9 us
  blocking collectives: 0 us -> 61.8 us
  loops' own time: 35 us -> 0 us
  local copies, waits for them, and re-layouts: 52.1 us -> 24 us
    ppermute x28 -> x0, starting transfers between devices: 1110 us -> none  [stage_and_hop(): received = lax.ppermute(state, 'sp', hop_pairs)]
    reduce_scatter x1 -> x0, waiting for transfers between devices: 560 us -> none  [local_fn(): lax.psum_scatter(partial_sum, 'hp', scatter_dimension=2, tiled=True)]
    ppermute x28 -> x0, waiting for transfers between devices: 468 us -> none  [stage_and_hop(): received = lax.ppermute(state, 'sp', hop_pairs)]
    dot_general x60 -> x4, matrix products: 213 us -> 12.2 us  [the longest x3 10.1 us: project(): p = jnp.dot(flat, theta, preferred_element_type=F32).astype(BF16)]
    pallas_call x0 -> x1, Pallas kernels: none -> 68.9 us  [run_chains(): pl.pallas_call(functools.partial(ttt_kernel, n_chains), out_shape=jax.Sha...]
    all_to_all x0 -> x2, blocking collectives: none -> 61.8 us  [the longest x1 47.6 us: local_fn(): w_cols = lax.all_to_all(w_out, 'hp', 1, 0, tiled=True)]
    select_n x28 -> x0, other arithmetic: 43.6 us -> none  [stage_and_hop(): jnp.where(take_new, new_val, old_val)]
    another operation x10 -> x0, loops' own time: 35 us -> none  [the longest x1 34 us: local_fn(): carry = lax.fori_loop(0, seq_size - 1, stage_and_hop, (start, empty_out))]
  transfers between devices with their start and end apart: 29 -> 2, of which waited for: 12 -> 1; matrix products, arithmetic and copies ran while one was open for 1% -> 8% of each run, Pallas kernels for 0% -> 0%
where the time goes in v1:
time: 203 us; the launch traced here: 202 us
  Pallas kernels  68.9 us (34%)
  blocking collectives  61.8 us (30%)
  local copies, waits for them, and re-layouts  24 us (12%)
  between operations  13.5 us (7%)
  waiting for transfers between devices  12.9 us (6%)
  matrix products  12.2 us (6%)
  starting transfers between devices  6.34 us (3%)
  other arithmetic  2.37 us (1%)
    pallas_call x1, Pallas kernels, run_chains(): pl.pallas_call(functools.partial(ttt_kernel, n_chains), out_shape=jax.Sha...  68.9 us
    all_to_all x1, blocking collectives, local_fn(): w_cols = lax.all_to_all(w_out, 'hp', 1, 0, tiled=True)  47.6 us
    all_to_all x1, blocking collectives, local_fn(): got = lax.all_to_all(got, 'sp', 0, 0, tiled=True)  14.3 us
    all_to_all x1, waiting for transfers between devices, local_fn(): kvq = lax.all_to_all(kvq, 'sp', 0, 0, tiled=True)  12.9 us
    dot_general x3, matrix products, project(): p = jnp.dot(flat, theta, preferred_element_type=F32).astype(BF16)  10.1 us
    all_to_all x1, starting transfers between devices, local_fn(): kvq = lax.all_to_all(kvq, 'sp', 0, 0, tiled=True)  6.34 us
    unnamed x7, local copies, waits for them, and re-layouts  5.52 us
    dynamic_slice x4, local copies, waits for them, and re-layouts, pick(): return lax.dynamic_index_in_dim(arr, head, 0, keepdims=False)  4.36 us
  transfers between devices with their start and end apart: 2, of which 1 were waited for; matrix products, arithmetic and copies ran while one was open for 8% of the time, Pallas kernels for 0%

profile of v1, /device:TPU:97, one launch (start us, length us, event | category | flops | bytes accessed | tf_op | source)
XLA Modules:
  0.0 202.0 jit_solution(1535574710878265126)
XLA Ops:
  6.5 0.0 copy-start
  6.6 1.6 copy-done
  8.1 2.8 %convolution_convert_fusion = bf16[512,512]{1,0:T(8,128)(2,1)S(1)} fusion(bf16[512,2048]{1,0:T(8,128)(2,1)S(1)} %bitcast.37, bf16[2048,512]{1,0:T(8,128)(2,1)} %param.13), kind=kOutput, calls=%fused_computation.5 | convolution fusion | flops 1074003968 | bytes 4718592 | tf_op jit(solution)/shard_map/dot_general | solution.py:206
  11.0 0.1 reshape.42
  11.1 0.1 copy.28
  11.2 3.6 %convolution_convert_fusion.1 = bf16[512,512]{1,0:T(8,128)(2,1)} fusion(bf16[512,2048]{1,0:T(8,128)(2,1)S(1)} %bitcast.36, bf16[2048,512]{1,0:T(8,128)(2,1)} %param.15), kind=kOutput, calls=%fused_computation.6 | convolution fusion | flops 1074003968 | bytes 4718592 | tf_op jit(solution)/shard_map/dot_general | solution.py:206
  14.9 1.2 reshape.40
  16.0 0.9 copy.27
  16.9 3.6 %convolution_convert_fusion.2 = bf16[512,512]{1,0:T(8,128)(2,1)} fusion(bf16[512,2048]{1,0:T(8,128)(2,1)S(1)} %bitcast.35, bf16[2048,512]{1,0:T(8,128)(2,1)} %param.14), kind=kOutput, calls=%fused_computation.7 | convolution fusion | flops 1074003968 | bytes 4718592 | tf_op jit(solution)/shard_map/dot_general | solution.py:206
  20.6 1.2 reshape.38
  21.7 0.1 copy.26
  21.8 2.4 %pad_maximum_fusion = bf16[8,2,3,128,128]{4,3,2,1,0:T(8,128)(2,1)} fusion(bf16[8,2,1,128,128]{4,3,2,1,0:T(8,128)(2,1)S(1)} %bitcast.44, bf16[8,2,1,128,128]{4,3,2,1,0:T(8,128)(2,1)} %bitcast.45, bf16[8,2,1,128,128]{4,3,2,1,0:T(8,128)(2,1)S(1)} %bitcast.46), kind=kLoop, calls=%fused_computation.3 | loop fusion | flops 1572864 | bytes 3145728 | tf_op jit(solution)/shard_map/concatenate | solution.py:210
  24.2 0.0 copy-start.2
  24.2 6.3 %all-to-all-start = ((bf16[8,2,3,128,128]{4,3,2,1,0:T(8,128)(2,1)}), bf16[8,2,3,128,128]{4,3,2,1,0:T(8,128)(2,1)}, u32[]{:S(2)}, u32[]{:S(2)}) async-start(bf16[8,2,3,128,128]{4,3,2,1,0:T(8,128)(2,1)} %pad_maximum_fusion), calls=%async_computation | async-start | bytes 3145728 | tf_op jit(solution)/shard_map/all_to_all | solution.py:211
  30.5 0.0 all-gather.2.cloned.1.call-start
  30.5 0.0 copy-done.2
  30.6 0.6 dynamic_slice.32
  31.1 1.3 constant_dynamic-slice_fusion.2.b2
  32.4 1.2 constant_dynamic-slice_fusion
  33.6 1.3 constant_dynamic-slice_fusion.3.b1
  34.9 1.7 dynamic-slice_bitcast_fusion.1.w1
  36.6 1.7 dynamic-slice_bitcast_fusion.w2
  38.3 12.9 %all-to-all-done.kvq = bf16[8,2,3,128,128]{4,3,2,1,0:T(8,128)(2,1)} async-done(((bf16[8,2,3,128,128]{4,3,2,1,0:T(8,128)(2,1)}), bf16[8,2,3,128,128]{4,3,2,1,0:T(8,128)(2,1)}, u32[]{:S(2)}, u32[]{:S(2)}) %all-to-all-start) | async-done | bytes 1572896 | tf_op jit(solution)/shard_map/all_to_all | solution.py:211
  51.1 68.9 %shard_map.118 = bf16[8,2,128,128]{3,2,1,0:T(8,128)(2,1)} custom-call(bf16[8,2,3,128,128]{4,3,2,1,0:T(8,128)(2,1)} %all-to-all-done.kvq, f32[128,512]{1,0:T(8,128)} %dynamic-slice_bitcast_fusion.1.w1, f32[1,512]{1,0:T(1,128)} %constant_dynamic-slice_fusion.3.b1, f32[512,128]{1,0:T(8,128)} %dynamic-slice_bitcast_fusion.w2, ...), custom_call_target="tpu_custom_call" | custom-call | tf_op jit(solution)/shard_map/pallas_call | solution.py:186
  120.0 14.3 %all_to_all.29 = bf16[8,2,128,128]{3,2,1,0:T(8,128)(2,1)} all-to-all(bf16[8,2,128,128]{3,2,1,0:T(8,128)(2,1)} %shard_map.118), channel_id=1, replica_groups=mesh['dp'=1,'hp'=4,'sp'=8] {'sp'}, dimensions={0} | all-to-all | bytes 1048576 | tf_op jit(solution)/shard_map/all_to_all | solution.py:221
  134.3 0.1 all-gather.2.cloned.1.call-update
  134.3 3.9 %copy.30 = bf16[512,2048]{0,1:T(8,128)(2,1)} copy(bf16[512,2048]{1,0:T(8,128)(2,1)} %param.16) | data formatting | bytes 4194304 | tf_op args[4]
  138.2 47.6 %all_to_all.30 = bf16[512,4,512]{0,2,1:T(8,128)(2,1)} all-to-all(bf16[512,4,512]{0,2,1:T(8,128)(2,1)} %bitcast.39), channel_id=1, replica_groups=mesh['dp'=1,'hp'=4,'sp'=8] {'hp'}, dimensions={1} | all-to-all | bytes 4194304 | tf_op jit(solution)/shard_map/all_to_all | solution.py:224
  185.8 4.1 %copy.31 = bf16[4,512,512]{2,1,0:T(8,128)(2,1)} copy(bf16[4,512,512]{1,2,0:T(8,128)(2,1)} %bitcast.38) | data formatting | bytes 4194304 | tf_op jit(solution)/shard_map/all_to_all | solution.py:224
  190.0 0.0 all-gather.2.cloned.1.call-done
  190.0 0.0 copy-start.1
  190.0 3.1 %copy.29 = bf16[4,128,16,128]{3,2,1,0:T(8,128)(2,1)S(1)} copy(bf16[4,128,16,128]{3,1,0,2:T(8,128)(2,1)} %bitcast.40) | data formatting | bytes 4194304 | tf_op jit(solution)/shard_map/transpose | solution.py:225
  193.1 0.0 copy-done.1
  193.1 2.1 %fusion.3 = bf16[512,512]{1,0:T(8,128)(2,1)} fusion(bf16[2048,512]{1,0:T(8,128)(2,1)S(1)} %bitcast.41, bf16[64,8,16,128]{3,2,1,0:T(8,128)(2,1)S(1)} %bitcast.42), kind=kOutput, calls=%fused_computation.4 | convolution fusion | flops 1074003968 | bytes 4718592 | tf_op jit(solution)/shard_map/dot_general | solution.py:226
Async XLA Ops:
  6.5 1.6 copy-start
  24.2 6.3 %copy-start.2 = (f32[4]{0:T(128)S(1)}, f32[4]{0:T(128)}, u32[]{:S(2)}) copy-start(f32[4]{0:T(128)} %param.23) | copy-start | bytes 52
  24.2 26.9 %all-to-all-start = ((bf16[8,2,3,128,128]{4,3,2,1,0:T(8,128)(2,1)}), bf16[8,2,3,128,128]{4,3,2,1,0:T(8,128)(2,1)}, u32[]{:S(2)}, u32[]{:S(2)}) async-start(bf16[8,2,3,128,128]{4,3,2,1,0:T(8,128)(2,1)} %pad_maximum_fusion), calls=%async_computation | async-start | bytes 3145728 | tf_op jit(solution)/shard_map/all_to_all | solution.py:211
  30.5 159.4 %all-gather.2.cloned.1.call-start = ((), (), s32[]{:S(2)}) async-start(), calls=%async_computation.3 | async-start | bytes 2621440 | tf_op jit(solution)/shard_map/all_gather | solution.py:223
  190.0 3.1 %copy-start.1 = (bf16[4,512,512]{2,1,0:T(8,128)(2,1)S(1)}, bf16[4,512,512]{2,1,0:T(8,128)(2,1)}, u32[]{:S(2)}) copy-start(bf16[4,512,512]{2,1,0:T(8,128)(2,1)} %copy.31) | copy-start | bytes 6291460
Sparse Core Ops, SparseCore 0:
  134.4 50.4 all-gather.1

commit v2 on v1

--- a/solution.py
+++ b/solution.py
@@ -41,18 +41,137 @@
     return [high, high, high, mid, mid, low]
 
 
-def ttt_kernel(n_chains, kvq, w1, b1, w2, b2, gamma, beta, rate, out, *scr):
-    n_blocks, block = kvq.shape[0], kvq.shape[3]
+MESH = pl.DeviceIdType.MESH
+PIECE = 2 * MINI
+CHAIN_REFS = 11
+
+
+def ttt_kernel(n_hp, n_sp, n_chains, tokens, theta_k, theta_v, theta_q, w_out, w_one, w_two, b_one, b_two, gammas, betas, rates,
+               res, tok, theta, wcols, kvq, send, outb, gath, w1, w2, in_sem, send_sem, recv_sem, wsend_sem, wrecv_sem,
+               osend_sem, orecv_sem, *scr):
+    batch, block, model = tokens.shape
+    heads, dim, hid = w_one.shape
+    n_pieces = block // PIECE
     per_block = block // MINI
-    n_steps = n_blocks * per_block
-    dim, hid = w1.shape
-    per = len(scr) // n_chains
-    chains = [scr[i * per:(i + 1) * per] for i in range(n_chains)]
-    factor = rate[0, 0] / MINI
-    gain, bias = gamma[...], beta[...]
+    per_piece = PIECE // MINI
+    n_steps = n_sp * per_block
+    cols = model // n_hp
+    rows = heads * dim
+    per_head = batch // n_chains
+    my_hp, me = lax.axis_index("hp"), lax.axis_index("sp")
+    linear = my_hp * n_sp + me
+    n_all = n_hp * n_sp
+    head = me // per_head
+    chains = [scr[i * CHAIN_REFS:(i + 1) * CHAIN_REFS] for i in range(n_chains)]
+    factor = rates[head] / MINI
+    gain, bias = gammas[pl.ds(head, 1), :], betas[pl.ds(head, 1), :]
+
+    def head_of(turn):
+        return lax.rem(head + turn, heads)
+
+    barrier = pltpu.get_barrier_semaphore()
+    for off in range(1, n_all):
+        other = lax.rem(linear + off, n_all)
+        pl.semaphore_signal(barrier, inc=1, device_id={"hp": other // n_sp, "sp": lax.rem(other, n_sp)}, device_id_type=MESH)
+
+    loads = []
+
+    def fetch(src, dst):
+        copy = pltpu.make_async_copy(src, dst, in_sem.at[len(loads)])
+        copy.start()
+        loads.append(copy)
+
+    turns = [[2, 1], [3, 0]]
+    for b in range(batch):
+        fetch(tokens.at[b], tok.at[pl.ds(b * block, block)])
+    for r, pair in enumerate(turns):
+        for u, turn in enumerate(pair):
+            where = pl.ds(pl.multiple_of(head_of(turn) * dim, dim), dim)
+            for i, part in enumerate((theta_k, theta_v, theta_q)):
+                fetch(part.at[:, where], theta.at[r, :, pl.ds((u * 3 + i) * dim, dim)])
+    fetch(w_one.at[head], w1)
+    fetch(w_two.at[head], w2)
+    mine = pl.ds(pl.multiple_of(my_hp * cols, cols), cols)
+    my_rows = pl.ds(pl.multiple_of(my_hp * rows, rows), rows)
+    fetch(w_out.at[:, mine], wcols.at[my_rows])
+
+    done = 0
+    for r, pair in enumerate(turns):
+        upto = batch + (r + 1) * 3 * len(pair)
+        for copy in loads[done:upto]:
+            copy.wait()
+        done = upto
+        p = dot(tok[...], theta[r]).astype(BF16)
+        for u, turn in enumerate(pair):
+            for b in range(batch):
+                dest = head_of(turn) * per_head + b // n_chains
+                for i in range(3):
+                    tile = p[b * block:(b + 1) * block, (u * 3 + i) * dim:(u * 3 + i + 1) * dim]
+                    for q in range(n_pieces):
+                        send[dest, q, b % n_chains, i] = tile[q * PIECE:(q + 1) * PIECE]
+    for copy in loads[done:]:
+        copy.wait()
+    kvq[me] = send[me]
+
+    pl.semaphore_wait(barrier, n_all - 1)
+
+    def kvq_copy(off, q):
+        dest = lax.rem(me + off, n_sp)
+        return pltpu.make_async_remote_copy(src_ref=send.at[dest, q], dst_ref=kvq.at[me, q], send_sem=send_sem.at[off, q],
+                                            recv_sem=recv_sem.at[me, q], device_id={"sp": dest}, device_id_type=MESH)
+
+    def send_all():
+        for q in range(n_pieces):
+            for off in range(1, n_sp):
+                kvq_copy(off, q).start()
+
+    def wait_piece(number):
+        src, q = number // n_pieces, lax.rem(number, n_pieces)
+
+        @pl.when(src != me)
+        def _():
+            pltpu.make_async_remote_copy(src_ref=send.at[0, q], dst_ref=kvq.at[src, q], send_sem=send_sem.at[0, q],
+                                         recv_sem=recv_sem.at[src, q], device_id={"sp": src}, device_id_type=MESH).wait_recv()
+
+    def w_copy(off):
+        dest = lax.rem(my_hp + off, n_hp)
+        return pltpu.make_async_remote_copy(
+            src_ref=w_out.at[:, pl.ds(pl.multiple_of(dest * cols, cols), cols)], dst_ref=wcols.at[my_rows],
+            send_sem=wsend_sem.at[off], recv_sem=wrecv_sem.at[off], device_id={"hp": dest}, device_id_type=MESH)
+
+    @pl.when(me == 0)
+    def _():
+        send_all()
+
+    for off in range(1, n_hp):
+        w_copy(off).start()
+
+    def send_out(number):
+        dest, q = number // n_pieces, lax.rem(number, n_pieces)
+
+        def start(off):
+            target = lax.rem(my_hp + off, n_hp)
+            pltpu.make_async_remote_copy(src_ref=outb.at[dest, q], dst_ref=gath.at[linear, q], send_sem=osend_sem,
+                                         recv_sem=orecv_sem, device_id={"hp": target, "sp": dest}, device_id_type=MESH).start()
+
+        for off in range(1, n_hp):
+            start(off)
+
+        @pl.when(dest != me)
+        def _():
+            start(0)
+
+        @pl.when(dest == me)
+        def _():
+            gath[linear, q] = outb[dest, q]
 
     def load(chain, which, step):
-        return kvq[step // per_block, chain, which, pl.ds(pl.multiple_of((step % per_block) * MINI, MINI), MINI), :]
+        piece = lax.rem(step, per_block)
+        return kvq[step // per_block, piece // per_piece, chain, which, pl.ds(pl.multiple_of(lax.rem(piece, per_piece) * MINI, MINI), MINI), :]
+
+    def store_out(chain, step, value):
+        piece = lax.rem(step, per_block)
+        outb[step // per_block, piece // per_piece, chain, pl.ds(pl.multiple_of(lax.rem(piece, per_piece) * MINI, MINI), MINI), :] = value.astype(BF16)
 
     def store_first(refs, value):
         w1f, w1hm, w1lo = refs
@@ -81,10 +200,15 @@
         w2t = w2[...].T
         w2t = w2t - jnp.mean(w2t, axis=0, keepdims=True)
         store_first((w2f, w2hm, w2lo), w2t)
-        b1r[...] = b1[...]
-        b2r[...] = b2[...] - jnp.mean(b2[...], axis=1, keepdims=True)
+        b1r[...] = b_one[pl.ds(head, 1), :]
+        b2 = b_two[pl.ds(head, 1), :]
+        b2r[...] = b2 - jnp.mean(b2, axis=1, keepdims=True)
         dh8[...] = jnp.zeros_like(dh8)
         cor[...] = jnp.zeros_like(cor)
+
+    wait_piece(0)
+    for c in range(n_chains):
+        w1f, w1hm, w1lo, w2f, w2hm, w2lo, b1r, b2r, zb, cor, dh8 = chains[c]
         zb[...] = base(jnp.concatenate([load(c, 2, 0), load(c, 0, 0)], axis=0), w1hm, w1lo, b1r)
 
     def step_chain(c, step):
@@ -125,8 +249,7 @@
         var = jnp.mean(yc * yc, axis=1, keepdims=True)
         rstd = lax.rsqrt(var + EPS)
         xhat = yc * rstd
-        out[before // per_block, c, pl.ds(pl.multiple_of((before % per_block) * MINI, MINI), MINI), :] = (
-            qry_f + gain * xhat[:MINI] + bias).astype(BF16)
+        store_out(c, before, qry_f + gain * xhat[:MINI] + bias)
 
         xk = xhat[MINI:]
         dx = (key_f + gain * xk + bias - val_f) * ((2.0 * factor) * gain)
@@ -152,6 +275,20 @@
         b1r[...] = b1r[...] - jnp.sum(dh, axis=0, keepdims=True)
 
     def body(step, carry):
+        after = step + 1
+
+        @pl.when((lax.rem(after, per_piece) == 0) & (after < n_steps))
+        def _():
+            wait_piece(after // per_piece)
+
+        @pl.when((me > 0) & (step == jnp.maximum(me - 2, 0) * per_block))
+        def _():
+            send_all()
+
+        @pl.when((lax.rem(step, per_piece) == 1) & (step > per_piece))
+        def _():
+            send_out((step - 1) // per_piece - 1)
+
         running = [step_chain(c, step) for c in range(n_chains)]
         while running:
             running = [g for g in running if next(g, 1) is None]
@@ -170,61 +307,74 @@
         r = r[:, :dim] + r[:, dim:]
         yc = r[:MINI] + r[MINI:2 * MINI] + r[2 * MINI:] + dot_t(hp[0], w2lo[...]) + b2r[...]
         xhat = yc * lax.rsqrt(jnp.mean(yc * yc, axis=1, keepdims=True) + EPS)
-        out[n_blocks - 1, c, pl.ds(block - MINI, MINI), :] = (qry.astype(F32) + gain * xhat + bias).astype(BF16)
-
-
-def run_chains(kvq, w1, b1, w2, b2, gamma, beta, rate):
-    n_blocks, n_chains, _, block, dim = kvq.shape
-    hid = w1.shape[1]
-    vmem = pl.BlockSpec(memory_space=pltpu.VMEM)
+        store_out(c, n_steps - 1, qry.astype(F32) + gain * xhat + bias)
+
+
+    send_out(n_sp * n_pieces - 1)
+    for off in range(1, n_hp):
+        w_copy(off).wait()
+    everyone = gath.at[pl.ds(0, n_all - 1)]
+    pltpu.make_async_copy(everyone, everyone, orecv_sem).wait()
+    total = None
+    for two in range(n_hp * heads // 2):
+        left = []
+        for one in (2 * two, 2 * two + 1):
+            parts = []
+            for b in range(batch):
+                chain = one * batch + b
+                parts += [gath[chain // n_chains, q, chain % n_chains] for q in range(n_pieces)]
+            left.append(jnp.concatenate(parts, axis=0))
+        term = dot(jnp.concatenate(left, axis=1), wcols[pl.ds(two * 2 * dim, 2 * dim), :])
+        total = term if total is None else total + term
+    total = total.astype(BF16)
+    for b in range(batch):
+        res[b] = total[b * block:(b + 1) * block]
+    pltpu.make_async_copy(everyone, everyone, osend_sem).wait()
+    for q in range(n_pieces):
+        for off in range(1, n_sp):
+            kvq_copy(off, q).wait_send()
+
+
+def run(n_hp, n_sp, tokens, theta_k, theta_v, theta_q, w_out, w_one, w_two, b_one, b_two, gammas, betas, rates):
+    batch, block, model = tokens.shape
+    heads, dim, hid = w_one.shape
+    n_chains = heads * batch // n_sp
+    assert batch % n_chains == 0 and heads % 2 == 0 and block % PIECE == 0
+    n_pieces = block // PIECE
+    n_all = n_hp * n_sp
+    cols = model // n_hp
+    any_ref, vmem = pl.BlockSpec(memory_space=pl.ANY), pl.BlockSpec(memory_space=pltpu.VMEM)
+    dma, v = pltpu.SemaphoreType.DMA, pltpu.VMEM
     per_chain = [
-        pltpu.VMEM((dim, hid), F32), pltpu.VMEM((2 * dim, hid), BF16), pltpu.VMEM((dim, hid), BF16),
-        pltpu.VMEM((dim, hid), F32), pltpu.VMEM((2 * dim, hid), BF16), pltpu.VMEM((dim, hid), BF16),
-        pltpu.VMEM((1, hid), F32), pltpu.VMEM((1, dim), F32), pltpu.VMEM((2 * MINI, hid), F32),
-        pltpu.VMEM((2 * MINI, 8 * MINI), BF16), pltpu.VMEM((8 * MINI, hid), BF16),
+        v((dim, hid), F32), v((2 * dim, hid), BF16), v((dim, hid), BF16),
+        v((dim, hid), F32), v((2 * dim, hid), BF16), v((dim, hid), BF16),
+        v((1, hid), F32), v((1, dim), F32), v((2 * MINI, hid), F32),
+        v((2 * MINI, 8 * MINI), BF16), v((8 * MINI, hid), BF16),
     ]
+    assert len(per_chain) == CHAIN_REFS
+    scratch = [
+        v((batch * block, model), BF16), v((2, model, heads // 2 * 3 * dim), BF16), v((n_hp * heads * dim, cols), BF16),
+        v((n_sp, n_pieces, n_chains, 3, PIECE, dim), BF16), v((n_sp, n_pieces, n_chains, 3, PIECE, dim), BF16),
+        v((n_sp, n_pieces, n_chains, PIECE, dim), BF16), v((n_all, n_pieces, n_chains, PIECE, dim), BF16),
+        v((dim, hid), F32), v((hid, dim), F32),
+        dma((batch + 3 * heads + 3,)), dma((n_sp, n_pieces)), dma((n_sp, n_pieces)), dma((n_hp,)), dma((n_hp,)), dma, dma,
+    ] + per_chain * n_chains
     return pl.pallas_call(
-        functools.partial(ttt_kernel, n_chains),
-        out_shape=jax.ShapeDtypeStruct((n_blocks, n_chains, block, dim), BF16),
-        in_specs=[vmem] * 7 + [pl.BlockSpec(memory_space=pltpu.SMEM)],
+        functools.partial(ttt_kernel, n_hp, n_sp, n_chains),
+        out_shape=jax.ShapeDtypeStruct((batch, block, cols), BF16),
+        in_specs=[any_ref] * 7 + [vmem] * 4 + [pl.BlockSpec(memory_space=pltpu.SMEM)],
         out_specs=vmem,
-        scratch_shapes=per_chain * n_chains,
-    )(kvq, w1, b1, w2, b2, gamma, beta, rate)
+        scratch_shapes=scratch,
+        compiler_params=pltpu.CompilerParams(collective_id=0, has_side_effects=True),
+    )(tokens, theta_k, theta_v, theta_q, w_out, w_one, w_two, b_one, b_two, gammas, betas, rates)
 
 
 def solution(mesh):
-    sp = mesh.shape["sp"]
-    hp = mesh.shape["hp"]
+    n_sp = mesh.shape["sp"]
+    n_hp = mesh.shape["hp"]
 
     def local_fn(tokens, theta_q, theta_k, theta_v, w_out, w_one, b_one, w_two, b_two, ln_gamma, ln_beta, inner_lr):
-        batch, block, model = tokens.shape
-        heads, dim = w_one.shape[0], w_one.shape[1]
-        n_chains = heads * batch // sp
-        flat = tokens.reshape(batch * block, model)
-
-        def project(theta):
-            p = jnp.dot(flat, theta, preferred_element_type=F32).astype(BF16)
-            p = p.reshape(batch, block, heads, dim).transpose(2, 0, 1, 3)
-            return p.reshape(sp, n_chains, 1, block, dim)
-
-        kvq = jnp.concatenate([project(theta_k), project(theta_v), project(theta_q)], axis=2)
-        kvq = lax.all_to_all(kvq, "sp", 0, 0, tiled=True)
-
-        first = lax.axis_index("sp") * n_chains
-        head = first // batch
-
-        def pick(arr):
-            return lax.dynamic_index_in_dim(arr, head, 0, keepdims=False)
-
-        got = run_chains(kvq, pick(w_one), pick(b_one)[None], pick(w_two), pick(b_two)[None], pick(ln_gamma)[None],
-                         pick(ln_beta)[None], pick(inner_lr).reshape(1, 1))
-        got = lax.all_to_all(got, "sp", 0, 0, tiled=True)
-        got = got.reshape(heads, batch, block, dim)
-        got = lax.all_gather(got, "hp", axis=0, tiled=True)
-        w_cols = lax.all_to_all(w_out, "hp", 1, 0, tiled=True)
-        rows = got.transpose(1, 2, 0, 3).reshape(batch * block, hp * heads * dim)
-        res = jnp.dot(rows, w_cols, preferred_element_type=F32).astype(BF16)
-        return res.reshape(batch, block, model // hp)
+        return run(n_hp, n_sp, tokens, theta_k, theta_v, theta_q, w_out, w_one, w_two, b_one, b_two, ln_gamma, ln_beta, inner_lr)
 
     head_spec = P("hp", None)
     cube_spec = P("hp", None, None)

time: 203 us -> 105 us (0.52)
  the two profiles are of different devices: /device:TPU:97 before, /device:TPU:103 now
where the time goes in v2:
time: 105 us
  Pallas kernels  103 us (98%)
  local copies, waits for them, and re-layouts  1.87 us (2%)
    pallas_call x1, Pallas kernels, run(): pl.pallas_call(functools.partial(ttt_kernel, n_hp, n_sp, n_chains), out_s...  103 us

profile of v2, /device:TPU:103, one launch (start us, length us, event | category | flops | bytes accessed | tf_op | source)
XLA Modules:
  0.0 105.0 jit_solution(3926460912053318695)
XLA Ops:
  0.0 103.1 %shard_map.118 = bf16[4,128,512]{2,1,0:T(8,128)(2,1)} custom-call(bf16[4,128,2048]{2,1,0:T(8,128)(2,1)} %tokens.1, bf16[2048,512]{1,0:T(8,128)(2,1)} %theta_k.1, bf16[2048,512]{1,0:T(8,128)(2,1)} %theta_v.1, bf16[2048,512]{1,0:T(8,128)(2,1)} %theta_q.1, bf16[512,2048]{1,0:T(8,128)(2,1)} %w_out.1, f32[4,128,512]{2,1,0:T(8,128)} %w_one.1, ...), custom_call_target="tpu_custom_call" | custom-call | tf_op jit(solution)/shard_map/pallas_call | solution.py:362
  103.1 1.9 %copy.14 = bf16[4,128,512]{2,1,0:T(8,128)(2,1)} copy(bf16[4,128,512]{2,1,0:T(8,128)(2,1)} %shard_map.118) | data formatting | bytes 1048576

commit v3 on v2

v3 whole, which is shorter than its diff:
```python
import functools

import jax
import jax.numpy as jnp
from jax import lax
from jax.experimental import pallas as pl
from jax.experimental.pallas import tpu as pltpu
from jax.sharding import PartitionSpec as P

MINI = 16
EPS = 1e-6
GELU_A = 0.7978845608028654
GELU_B = 0.044715
F32 = jnp.float32
BF16 = jnp.bfloat16


def split3(x):
    high = x.astype(BF16)
    rest = x - high.astype(F32)
    mid = rest.astype(BF16)
    low = (rest - mid.astype(F32)).astype(BF16)
    return high, mid, low


def dot(a, b):
    return jnp.dot(a, b, preferred_element_type=F32)


def dot_t(a, b):
    return lax.dot_general(a, b, (((1,), (1,)), ((), ())), preferred_element_type=F32)


def six(parts):
    high, mid, low = parts
    return [high, mid, low, high, mid, high]


def six_other(parts):
    high, mid, low = parts
    return [high, high, high, mid, mid, low]


MESH = pl.DeviceIdType.MESH
PIECE = 2 * MINI
CHAIN_REFS = 14
TURNS = [[2, 1], [3, 0]]
ORDER = ("A corr", "B y", "A w2", "B base", "A gelu", "A w1", "B ln", "A y", "B dh", "B w2", "A base", "B end", "A ln",
         "B corr", "B w1", "A dh", "B gelu", "A end")
PACE = 4
SHARE_LAG = 14
GROUP_LAG = 28
DIRECT = 2
W_STEP = 0


def ttt_kernel(n_hp, n_sp, n_chains, tokens, theta_k, theta_v, theta_q, w_out, w_one, w_two, b_one, b_two, gammas, betas, rates,
               res, tok, theta, wcols, kvq, send, outb, gath, made, resb, w1, w2, in_sem, send_sem, recv_sem, wsend_sem,
               wrecv_sem, osend_sem, orecv_sem, ssend_sem, srecv_sem, rsend_sem, rrecv_sem, ready_sem, *scr):
    batch, block, model = tokens.shape
    heads, dim, hid = w_one.shape
    n_pieces = block // PIECE
    per_block = block // MINI
    per_piece = PIECE // MINI
    n_steps = n_sp * per_block
    cols = model // n_hp
    rows = heads * dim
    per_head = batch // n_chains
    my_hp, me = lax.axis_index("hp"), lax.axis_index("sp")
    linear = my_hp * n_sp + me
    n_all = n_hp * n_sp
    head = me // per_head
    chains = [scr[i * CHAIN_REFS:(i + 1) * CHAIN_REFS] for i in range(n_chains)]
    factor = rates[head] / MINI
    gain, bias = gammas[pl.ds(head, 1), :], betas[pl.ds(head, 1), :]

    def head_of(turn):
        return lax.rem(head + turn, heads)

    barrier = pltpu.get_barrier_semaphore()
    for off in range(1, n_sp):
        pl.semaphore_signal(barrier, inc=1, device_id={"sp": lax.rem(me + off, n_sp)}, device_id_type=MESH)
    for off in range(1, n_hp):
        pl.semaphore_signal(barrier, inc=1, device_id={"hp": lax.rem(my_hp + off, n_hp)}, device_id_type=MESH)

    loads = []

    def fetch(src, dst):
        copy = pltpu.make_async_copy(src, dst, in_sem.at[len(loads)])
        copy.start()
        loads.append(copy)

    for b in range(batch):
        fetch(tokens.at[b], tok.at[pl.ds(b * block, block)])
    for r, pair in enumerate(TURNS):
        for u, turn in enumerate(pair):
            where = pl.ds(pl.multiple_of(head_of(turn) * dim, dim), dim)
            for i, part in enumerate((theta_k, theta_v, theta_q)):
                fetch(part.at[:, where], theta.at[r, :, pl.ds((u * 3 + i) * dim, dim)])
    fetch(w_one.at[head], w1)
    fetch(w_two.at[head], w2)
    mine = pl.ds(pl.multiple_of(my_hp * cols, cols), cols)
    my_rows = pl.ds(pl.multiple_of(my_hp * rows, rows), rows)
    fetch(w_out.at[:, mine], wcols.at[my_rows])

    half = n_sp // 2
    chip, core = me // 2, lax.rem(me, 2)

    def kvq_copy(delta, other, q, size):
        dest = lax.rem(chip + delta, half) * 2 + lax.rem(core + other, 2)
        return pltpu.make_async_remote_copy(
            src_ref=send.at[dest, pl.ds(q, size)], dst_ref=kvq.at[me, pl.ds(q, size)], send_sem=send_sem.at[2 * delta + other, q],
            recv_sem=recv_sem.at[me, q], device_id={"sp": dest}, device_id_type=MESH)

    kinds = [(me == 0, 1), (me == 1, 1), ((me > 1) & (me < half), 2), (me >= half, n_pieces)]

    def copies(which, deltas):
        size = kinds[which][1]
        return [kvq_copy(delta, other, q, size) for q in range(0, n_pieces, size) for delta in deltas for other in (0, 1)
                if delta + other > 0]

    def send_some(which, deltas, gate):
        @pl.when(kinds[which][0] & gate)
        def _():
            for copy in copies(which, deltas):
                copy.start()

    done = 0
    for r, pair in enumerate(TURNS):
        upto = batch + (r + 1) * 3 * len(pair)
        for copy in loads[done:upto]:
            copy.wait()
        done = upto
        p = dot(tok[...], theta[r]).astype(BF16)
        for u, turn in enumerate(pair):
            for b in range(batch):
                dest = head_of(turn) * per_head + b // n_chains
                for i in range(3):
                    tile = p[b * block:(b + 1) * block, (u * 3 + i) * dim:(u * 3 + i + 1) * dim]
                    for q in range(n_pieces):
                        send[dest, q, b % n_chains, i] = tile[q * PIECE:(q + 1) * PIECE]
        if r == 0:
            pl.semaphore_wait(barrier, n_sp + n_hp - 2)
            for off in range(1, n_hp):
                pl.semaphore_signal(ready_sem, inc=1, device_id={"hp": lax.rem(my_hp + off, n_hp)}, device_id_type=MESH)
        send_some(0, pair, me == 0)
    for copy in loads[done:]:
        copy.wait()
    kvq[me] = send[me]

    def wait_piece(number):
        src, q = number // n_pieces, lax.rem(number, n_pieces)

        def wait(size):
            pltpu.make_async_remote_copy(
                src_ref=send.at[0, pl.ds(q, size)], dst_ref=kvq.at[src, pl.ds(q, size)], send_sem=send_sem.at[0, q],
                recv_sem=recv_sem.at[src, q], device_id={"sp": src}, device_id_type=MESH).wait_recv()

        @pl.when((src != me) & (src < 2))
        def _():
            wait(1)

        @pl.when((src != me) & (src > 1) & (src < half) & (lax.rem(q, 2) == 0))
        def _():
            wait(2)

        @pl.when((src != me) & (src >= half) & (q == 0))
        def _():
            wait(n_pieces)

    def w_copy(off):
        dest = lax.rem(my_hp + off, n_hp)
        return pltpu.make_async_remote_copy(
            src_ref=w_out.at[:, pl.ds(pl.multiple_of(dest * cols, cols), cols)], dst_ref=wcols.at[my_rows],
            send_sem=wsend_sem.at[off], recv_sem=wrecv_sem.at[off], device_id={"hp": dest}, device_id_type=MESH)

    for off in range(1, n_hp):
        w_copy(off).start()

    def worker_of(turn):
        return lax.rem(turn, half) * 2 + turn // half

    my_turn = me // 2 + half * lax.rem(me, 2)
    n_groups = n_steps // per_piece // n_sp
    last = n_groups - 1
    first_direct = n_groups - DIRECT
    my_slots = pl.ds(pl.multiple_of(my_hp * n_sp, n_sp), n_sp)

    def send_out(number, spread):
        group, dest = number // n_sp, worker_of(lax.rem(number, n_sp))

        def start(off):
            target = lax.rem(my_hp + off, n_hp)
            pltpu.make_async_remote_copy(
                src_ref=outb.at[number], dst_ref=gath.at[group, linear], send_sem=osend_sem.at[int(spread)],
                recv_sem=orecv_sem.at[group], device_id={"hp": target, "sp": dest},
                device_id_type=MESH).start()

        if spread:
            for off in range(1, n_hp):
                start(off)

        @pl.when(dest != me)
        def _():
            start(0)

        @pl.when(dest == me)
        def _():
            gath[group, linear] = outb[number]

    def share_copy(group, off):
        return pltpu.make_async_remote_copy(
            src_ref=gath.at[group, my_slots], dst_ref=gath.at[group, my_slots], send_sem=ssend_sem, recv_sem=srecv_sem.at[group],
            device_id={"hp": lax.rem(my_hp + off, n_hp)}, device_id_type=MESH)

    def share_group(group):
        others = gath.at[group, pl.ds(0, n_sp - 1)]
        pltpu.make_async_copy(others, others, orecv_sem.at[group]).wait()
        for off in range(1, n_hp):
            share_copy(group, off).start()

    def result_copy(group):
        number = group * n_sp + my_turn
        owner, q = number // n_pieces, lax.rem(number, n_pieces)
        return owner, q, pltpu.make_async_remote_copy(
            src_ref=made.at[group], dst_ref=resb.at[q], send_sem=rsend_sem.at[group], recv_sem=rrecv_sem.at[q],
            device_id={"sp": owner}, device_id_type=MESH)

    def make_group(group):
        left = []
        for one in range(n_hp * heads):
            chain = [one * batch + b for b in range(batch)]
            left.append(jnp.concatenate([gath[group, c // n_chains, c % n_chains] for c in chain], axis=0))
        made[group] = dot(jnp.concatenate(left, axis=1), wcols[...]).astype(BF16).reshape(batch, PIECE, cols)
        owner, q, copy = result_copy(group)

        @pl.when(owner != me)
        def _():
            copy.start()

        @pl.when(owner == me)
        def _():
            resb[q] = made[group]

    def load(chain, which, step):
        piece = lax.rem(step, per_block)
        return kvq[step // per_block, piece // per_piece, chain, which, pl.ds(pl.multiple_of(lax.rem(piece, per_piece) * MINI, MINI), MINI), :]

    def store_out(chain, step, value):
        outb[step // per_piece, chain, pl.ds(pl.multiple_of(lax.rem(step, per_piece) * MINI, MINI), MINI), :] = value.astype(BF16)

    def store_first(refs, value):
        w1f, w1hm, w1lo = refs
        high, mid, low = split3(value)
        w1f[...] = value
        w1hm[:dim] = high
        w1hm[dim:] = mid
        w1lo[...] = low

    def correction(x, keys):
        rep = jnp.concatenate([keys] * 8, axis=0)
        a = dot_t(x, rep) + 1.0
        high, mid, low = split3(a)
        lane = lax.broadcasted_iota(jnp.int32, a.shape, 1)
        part = jnp.where(lane < 3 * MINI, high.astype(F32), jnp.where(lane < 5 * MINI, mid.astype(F32), low.astype(F32)))
        return jnp.where(lane < 6 * MINI, part, 0.0).astype(BF16)

    def base(x, w1hm, w1lo, b1r):
        return dot(jnp.concatenate([x, x], axis=1), w1hm[...]) + dot(x, w1lo[...]) + b1r[...]

    zeros32 = jnp.zeros((2 * MINI, hid), BF16)

    def hidden_in(c):
        return chains[c][8][...] - dot(chains[c][9][...], chains[c][10][...])

    def activate(c, z):
        w1f, w1hm, w1lo, w2f, w2hm, w2lo, b1r, b2r, zb, cor, dh8, hps, slope, d3r = chains[c]
        z2 = z * z
        t = jnp.tanh(z * (GELU_A + (GELU_A * GELU_B) * z2))
        cdf = 0.5 + 0.5 * t
        hps[...] = jnp.concatenate(split3(z * cdf), axis=0)
        zk, z2k, tk = z[MINI:], z2[MINI:], t[MINI:]
        slope[...] = cdf[MINI:] + (0.5 * zk * (1.0 - tk * tk)) * (GELU_A + (3.0 * GELU_A * GELU_B) * z2k)

    def update_first(c, step):
        w1f, w1hm, w1lo, w2f, w2hm, w2lo, b1r, b2r, zb, cor, dh8, hps, slope, d3r = chains[c]
        keys_t = jnp.concatenate([load(c, 0, step)] * 3 + [jnp.zeros((5 * MINI, dim), BF16)], axis=0).T
        store_first((w1f, w1hm, w1lo), w1f[...] - dot(keys_t, dh8[...]))

    def prepare(c, step):
        w1f, w1hm, w1lo, w2f, w2hm, w2lo, b1r, b2r, zb, cor, dh8, hps, slope, d3r = chains[c]
        x = jnp.concatenate([load(c, 2, step), load(c, 0, jnp.minimum(step + 1, n_steps - 1))], axis=0)
        zb[...] = base(x, w1hm, w1lo, b1r)
        cor[...] = correction(x, load(c, 0, step))

    def second_layer(c):
        w1f, w1hm, w1lo, w2f, w2hm, w2lo, b1r, b2r, zb, cor, dh8, hps, slope, d3r = chains[c]
        return dot_t(hps[...], w2hm[...]), dot_t(hps[:2 * MINI], w2lo[...])

    def normalised(c, r, yl):
        n2 = 2 * MINI
        r = r[:, :dim] + r[:, dim:]
        yc = r[:n2] + r[n2:2 * n2] + r[2 * n2:] + yl + chains[c][7][...]
        rstd = lax.rsqrt(jnp.mean(yc * yc, axis=1, keepdims=True) + EPS)
        return yc * rstd, rstd

    def residual(c, step, r, yl):
        w1f, w1hm, w1lo, w2f, w2hm, w2lo, b1r, b2r, zb, cor, dh8, hps, slope, d3r = chains[c]
        before = jnp.maximum(step - 1, 0)
        xhat, rstd = normalised(c, r, yl)
        store_out(c, before, load(c, 2, before).astype(F32) + gain * xhat[:MINI] + bias)
        xk = xhat[MINI:]
        dx = (load(c, 0, step).astype(F32) + gain * xk + bias - load(c, 1, step).astype(F32)) * ((2.0 * factor) * gain)
        m1 = jnp.mean(dx, axis=1, keepdims=True)
        m2 = jnp.mean(dx * xk, axis=1, keepdims=True)
        dy = rstd[MINI:] * (dx - m1 - xk * m2)
        d3r[...] = jnp.concatenate(split3(dy), axis=0)
        b2r[...] = b2r[...] - jnp.sum(dy, axis=0, keepdims=True)

    def back_dots(c):
        w1f, w1hm, w1lo, w2f, w2hm, w2lo, b1r, b2r, zb, cor, dh8, hps, slope, d3r = chains[c]
        d3 = d3r[...]
        return dot(jnp.concatenate([d3, d3], axis=1), w2hm[...]), dot(d3[:MINI], w2lo[...])

    def back_end(c, e, el):
        w1f, w1hm, w1lo, w2f, w2hm, w2lo, b1r, b2r, zb, cor, dh8, hps, slope, d3r = chains[c]
        dh = (e[:MINI] + e[MINI:2 * MINI] + e[2 * MINI:] + el) * slope[...]
        dh8[:6 * MINI] = jnp.concatenate(six(split3(dh)), axis=0)
        b1r[...] = b1r[...] - jnp.sum(dh, axis=0, keepdims=True)

    def update_second(c):
        w1f, w1hm, w1lo, w2f, w2hm, w2lo, b1r, b2r, zb, cor, dh8, hps, slope, d3r = chains[c]
        parts = [hps[(2 * i + 1) * MINI:(2 * i + 2) * MINI] for i in range(3)]
        hk8 = jnp.concatenate(six(parts) + [zeros32], axis=0)
        dyp = [d3r[i * MINI:(i + 1) * MINI] for i in range(3)]
        dy_t = jnp.concatenate(six_other(dyp) + [jnp.zeros((2 * MINI, dim), BF16)], axis=0).T
        store_first((w2f, w2hm, w2lo), w2f[...] - dot(dy_t, hk8))

    def one_step(step):
        ev = [c for c in range(n_chains) if c % 2 == 0]
        od = [c for c in range(n_chains) if c % 2 == 1]
        before = jnp.maximum(step - 1, 0)
        held = {}
        for part in ORDER:
            for c in (ev if part[0] == "A" else od):
                name = part[2:]
                if name == "corr":
                    held[c, "z"] = hidden_in(c)
                elif name == "gelu":
                    activate(c, held[c, "z"])
                elif name == "w1":
                    update_first(c, before if part[0] == "A" else step)
                elif name == "base":
                    prepare(c, step)
                elif name == "y":
                    held[c, "y"] = second_layer(c)
                elif name == "ln":
                    residual(c, step, *held[c, "y"])
                elif name == "dh":
                    held[c, "e"] = back_dots(c)
                elif name == "end":
                    back_end(c, *held[c, "e"])
                elif name == "w2":
                    update_second(c)

    for c in range(n_chains):
        w1f, w1hm, w1lo, w2f, w2hm, w2lo, b1r, b2r, zb, cor, dh8, hps, slope, d3r = chains[c]
        store_first((w1f, w1hm, w1lo), w1[...])
        w2t = w2[...].T
        w2t = w2t - jnp.mean(w2t, axis=0, keepdims=True)
        store_first((w2f, w2hm, w2lo), w2t)
        b1r[...] = b_one[pl.ds(head, 1), :]
        b2 = b_two[pl.ds(head, 1), :]
        b2r[...] = b2 - jnp.mean(b2, axis=1, keepdims=True)
        dh8[...] = jnp.zeros_like(dh8)
        cor[...] = jnp.zeros_like(cor)
        hps[...] = jnp.zeros_like(hps)
        d3r[...] = jnp.zeros_like(d3r)

    wait_piece(0)
    for c in range(n_chains):
        w1f, w1hm, w1lo, w2f, w2hm, w2lo, b1r, b2r, zb, cor, dh8, hps, slope, d3r = chains[c]
        zb[...] = base(jnp.concatenate([load(c, 2, 0), load(c, 0, 0)], axis=0), w1hm, w1lo, b1r)
        if c % 2 == 1:
            activate(c, hidden_in(c))

    def take_turns(running):
        while running:
            running = [g for g in running if next(g, 1) is None]

    def body(step, carry):
        after = step + 1

        @pl.when((lax.rem(after, per_piece) == 0) & (after < n_steps))
        def _():
            wait_piece(after // per_piece)

        send_some(1, (2, 3, 0), step == 0)
        send_some(1, (1,), step == PACE)
        send_some(2, (2, 1, 3, 0), step == (me - 1) * PACE)
        send_some(3, (2, 1, 3, 0), step == (me - half + 1) * PACE)

        number = (step - 1) // per_piece - 1
        finished = (lax.rem(step, per_piece) == 1) & (step > per_piece)

        @pl.when(finished & (number < first_direct * n_sp))
        def _():
            send_out(number, False)

        @pl.when(finished & (number >= first_direct * n_sp))
        def _():
            send_out(number, True)

        period = n_sp * per_piece
        since_share = step - SHARE_LAG - per_piece * my_turn
        since_group = step - GROUP_LAG - per_piece * my_turn

        @pl.when((since_share >= 0) & (since_share < first_direct * period) & (lax.rem(since_share, period) == 0))
        def _():
            share_group(since_share // period)

        @pl.when(step == GROUP_LAG)
        def _():
            for off in range(1, n_hp):
                w_copy(off).wait_recv()
            pl.semaphore_wait(ready_sem, n_hp - 1)

        @pl.when((since_group >= 0) & (since_group < first_direct * period) & (lax.rem(since_group, period) == 0))
        def _():
            group = since_group // period
            others = gath.at[group, pl.ds(0, n_all - n_sp)]
            pltpu.make_async_copy(others, others, srecv_sem.at[group]).wait()
            make_group(group)

        one_step(step)
        return carry

    lax.fori_loop(0, n_steps, body, 0)

    def last_output(c):
        if c % 2 == 0:
            z = hidden_in(c)
            update_second(c)
            yield
            activate(c, z)
        yield
        r, yl = second_layer(c)
        yield
        xhat, _ = normalised(c, r, yl)
        store_out(c, n_steps - 1, load(c, 2, n_steps - 1).astype(F32) + gain * xhat[:MINI] + bias)

    take_turns([last_output(c) for c in range(n_chains)])
    send_out(n_groups * n_sp - 1, True)
    for group in range(first_direct, n_groups):
        spread = gath.at[group, pl.ds(0, n_all - 1)]
        pltpu.make_async_copy(spread, spread, orecv_sem.at[group]).wait()
        make_group(group)

    for q in range(n_pieces):
        @pl.when(q != lax.rem(my_turn, n_pieces))
        def _():
            pltpu.make_async_copy(resb.at[q], resb.at[q], rrecv_sem.at[q]).wait()

        for b in range(batch):
            res[b, q * PIECE:(q + 1) * PIECE] = resb[q, b]

    for group in range(n_groups):
        owner, q, copy = result_copy(group)

        @pl.when(owner != me)
        def _():
            copy.wait_send()

    sent = outb.at[pl.ds(0, first_direct * (n_sp - 1))]
    pltpu.make_async_copy(sent, sent, osend_sem.at[0]).wait()
    sent = gath.at[pl.ds(0, DIRECT), pl.ds(0, n_all - 1)]
    pltpu.make_async_copy(sent, sent, osend_sem.at[1]).wait()
    shared = gath.at[pl.ds(0, first_direct), pl.ds(0, n_all - n_sp)]
    pltpu.make_async_copy(shared, shared, ssend_sem).wait()
    for off in range(1, n_hp):
        w_copy(off).wait_send()
    for which, (cond, size) in enumerate(kinds):
        @pl.when(cond)
        def _():
            for copy in copies(which, (0, 1, 2, 3)):
                copy.wait_send()


def run(n_hp, n_sp, tokens, theta_k, theta_v, theta_q, w_out, w_one, w_two, b_one, b_two, gammas, betas, rates):
    batch, block, model = tokens.shape
    heads, dim, hid = w_one.shape
    n_chains = heads * batch // n_sp
    assert batch % n_chains == 0 and heads % 2 == 0 and block % PIECE == 0
    n_pieces = block // PIECE
    n_all = n_hp * n_sp
    n_groups = n_pieces
    cols = model // n_hp
    any_ref, vmem = pl.BlockSpec(memory_space=pl.ANY), pl.BlockSpec(memory_space=pltpu.VMEM)
    dma, v = pltpu.SemaphoreType.DMA, pltpu.VMEM
    per_chain = [
        v((dim, hid), F32), v((2 * dim, hid), BF16), v((dim, hid), BF16),
        v((dim, hid), F32), v((2 * dim, hid), BF16), v((dim, hid), BF16),
        v((1, hid), F32), v((1, dim), F32), v((2 * MINI, hid), F32),
        v((2 * MINI, 8 * MINI), BF16), v((8 * MINI, hid), BF16),
        v((6 * MINI, hid), BF16), v((MINI, hid), F32), v((3 * MINI, dim), BF16),
    ]
    assert len(per_chain) == CHAIN_REFS
    scratch = [
        v((batch * block, model), BF16), v((2, model, heads // 2 * 3 * dim), BF16), v((n_hp * heads * dim, cols), BF16),
        v((n_sp, n_pieces, n_chains, 3, PIECE, dim), BF16), v((n_sp, n_pieces, n_chains, 3, PIECE, dim), BF16),
        v((n_sp * n_pieces, n_chains, PIECE, dim), BF16), v((n_groups, n_all, n_chains, PIECE, dim), BF16),
        v((n_groups, batch, PIECE, cols), BF16), v((n_pieces, batch, PIECE, cols), BF16),
        v((dim, hid), F32), v((hid, dim), F32),
        dma((batch + 3 * heads + 3,)), dma((n_sp, n_pieces)), dma((n_sp, n_pieces)), dma((n_hp,)), dma((n_hp,)), dma((2,)),
        dma((n_groups,)), dma, dma((n_groups,)), dma((n_groups,)), dma((n_pieces,)), pltpu.SemaphoreType.REGULAR,
    ] + per_chain * n_chains
    return pl.pallas_call(
        functools.partial(ttt_kernel, n_hp, n_sp, n_chains),
        out_shape=jax.ShapeDtypeStruct((batch, block, cols), BF16),
        in_specs=[any_ref] * 7 + [vmem] * 4 + [pl.BlockSpec(memory_space=pltpu.SMEM)],
        out_specs=vmem,
        scratch_shapes=scratch,
        compiler_params=pltpu.CompilerParams(collective_id=0, has_side_effects=True),
    )(tokens, theta_k, theta_v, theta_q, w_out, w_one, w_two, b_one, b_two, gammas, betas, rates)


def solution(mesh):
    n_sp = mesh.shape["sp"]
    n_hp = mesh.shape["hp"]

    def local_fn(tokens, theta_q, theta_k, theta_v, w_out, w_one, b_one, w_two, b_two, ln_gamma, ln_beta, inner_lr):
        return run(n_hp, n_sp, tokens, theta_k, theta_v, theta_q, w_out, w_one, w_two, b_one, b_two, ln_gamma, ln_beta, inner_lr)

    head_spec = P("hp", None)
    cube_spec = P("hp", None, None)
    col_spec = P(None, "hp")
    return jax.shard_map(local_fn, mesh=mesh, in_specs=(P("dp", "sp", None), col_spec, col_spec, col_spec, head_spec, cube_spec, head_spec, cube_spec, head_spec, head_spec, head_spec, P("hp")), out_specs=P("dp", "sp", "hp"), check_vma=False)
```

time: 105 us -> 100 us (0.952)
  Pallas kernels: 103 us -> 98.1 us
    pallas_call x1, Pallas kernels: 103 us -> 98.1 us  [run(): pl.pallas_call(functools.partial(ttt_kernel, n_hp, n_sp, n_chains), out_s...]
where the time goes in v3:
time: 100 us
  Pallas kernels  98.1 us (98%)
  local copies, waits for them, and re-layouts  1.87 us (2%)
    pallas_call x1, Pallas kernels, run(): pl.pallas_call(functools.partial(ttt_kernel, n_hp, n_sp, n_chains), out_s...  98.1 us

profile of v3, /device:TPU:103, one launch (start us, length us, event | category | flops | bytes accessed | tf_op | source)
XLA Modules:
  0.0 100.0 jit_solution(16415808993964074356)
XLA Ops:
  0.0 98.1 %shard_map.118 = bf16[4,128,512]{2,1,0:T(8,128)(2,1)} custom-call(bf16[4,128,2048]{2,1,0:T(8,128)(2,1)} %tokens.1, bf16[2048,512]{1,0:T(8,128)(2,1)} %theta_k.1, bf16[2048,512]{1,0:T(8,128)(2,1)} %theta_v.1, bf16[2048,512]{1,0:T(8,128)(2,1)} %theta_q.1, bf16[512,2048]{1,0:T(8,128)(2,1)} %w_out.1, f32[4,128,512]{2,1,0:T(8,128)} %w_one.1, ...), custom_call_target="tpu_custom_call" | custom-call | tf_op jit(solution)/shard_map/pallas_call | solution.py:517
  98.1 1.9 %copy.14 = bf16[4,128,512]{2,1,0:T(8,128)(2,1)} copy(bf16[4,128,512]{2,1,0:T(8,128)(2,1)} %shard_map.118) | data formatting | bytes 1048576

commit v4 on v3

--- a/solution.py
+++ b/solution.py
@@ -45,12 +45,12 @@
 PIECE = 2 * MINI
 CHAIN_REFS = 14
 TURNS = [[2, 1], [3, 0]]
-ORDER = ("A corr", "B y", "A w2", "B base", "A gelu", "A w1", "B ln", "A y", "B dh", "B w2", "A base", "B end", "A ln",
-         "B corr", "B w1", "A dh", "B gelu", "A end")
+ORDER = ("B w1s", "B y", "A w2f", "A corr", "A gelu", "A w1f", "A y", "B base", "B ln", "B dh", "A base", "B end",
+         "A ln", "B w2f", "B corr", "B w1", "A dh", "B gelu", "A end")
 PACE = 4
-SHARE_LAG = 14
-GROUP_LAG = 28
-DIRECT = 2
+SHARE_LAG = 16
+GROUP_LAG = 40
+DIRECT = 3
 W_STEP = 0
 
 
@@ -186,13 +186,13 @@
     first_direct = n_groups - DIRECT
     my_slots = pl.ds(pl.multiple_of(my_hp * n_sp, n_sp), n_sp)
 
-    def send_out(number, spread):
+    def send_out(number, spread, rows=pl.ds(0, PIECE)):
         group, dest = number // n_sp, worker_of(lax.rem(number, n_sp))
 
         def start(off):
             target = lax.rem(my_hp + off, n_hp)
             pltpu.make_async_remote_copy(
-                src_ref=outb.at[number], dst_ref=gath.at[group, linear], send_sem=osend_sem.at[int(spread)],
+                src_ref=outb.at[number, :, rows], dst_ref=gath.at[group, linear, :, rows], send_sem=osend_sem.at[int(spread)],
                 recv_sem=orecv_sem.at[group], device_id={"hp": target, "sp": dest},
                 device_id_type=MESH).start()
 
@@ -206,7 +206,7 @@
 
         @pl.when(dest == me)
         def _():
-            gath[group, linear] = outb[number]
+            gath[group, linear, :, rows] = outb[number, :, rows]
 
     def share_copy(group, off):
         return pltpu.make_async_remote_copy(
@@ -249,13 +249,15 @@
     def store_out(chain, step, value):
         outb[step // per_piece, chain, pl.ds(pl.multiple_of(lax.rem(step, per_piece) * MINI, MINI), MINI), :] = value.astype(BF16)
 
-    def store_first(refs, value):
-        w1f, w1hm, w1lo = refs
+    def spread_parts(full, pair, low_part):
+        store_parts((full, pair, low_part), full[...])
+
+    def store_parts(refs, value):
+        full, pair, low_part = refs
         high, mid, low = split3(value)
-        w1f[...] = value
-        w1hm[:dim] = high
-        w1hm[dim:] = mid
-        w1lo[...] = low
+        pair[:dim] = high
+        pair[dim:] = mid
+        low_part[...] = low
 
     def correction(x, keys):
         rep = jnp.concatenate([keys] * 8, axis=0)
@@ -285,7 +287,7 @@
     def update_first(c, step):
         w1f, w1hm, w1lo, w2f, w2hm, w2lo, b1r, b2r, zb, cor, dh8, hps, slope, d3r = chains[c]
         keys_t = jnp.concatenate([load(c, 0, step)] * 3 + [jnp.zeros((5 * MINI, dim), BF16)], axis=0).T
-        store_first((w1f, w1hm, w1lo), w1f[...] - dot(keys_t, dh8[...]))
+        return (w1f, w1hm, w1lo), w1f[...] - dot(keys_t, dh8[...])
 
     def prepare(c, step):
         w1f, w1hm, w1lo, w2f, w2hm, w2lo, b1r, b2r, zb, cor, dh8, hps, slope, d3r = chains[c]
@@ -334,7 +336,7 @@
         hk8 = jnp.concatenate(six(parts) + [zeros32], axis=0)
         dyp = [d3r[i * MINI:(i + 1) * MINI] for i in range(3)]
         dy_t = jnp.concatenate(six_other(dyp) + [jnp.zeros((2 * MINI, dim), BF16)], axis=0).T
-        store_first((w2f, w2hm, w2lo), w2f[...] - dot(dy_t, hk8))
+        return (w2f, w2hm, w2lo), w2f[...] - dot(dy_t, hk8)
 
     def one_step(step):
         ev = [c for c in range(n_chains) if c % 2 == 0]
@@ -348,8 +350,15 @@
                     held[c, "z"] = hidden_in(c)
                 elif name == "gelu":
                     activate(c, held[c, "z"])
-                elif name == "w1":
-                    update_first(c, before if part[0] == "A" else step)
+                elif name in ("w1", "w1f"):
+                    refs, value = update_first(c, before if part[0] == "A" else step)
+                    refs[0][...] = value
+                    if name == "w1f":
+                        store_parts(refs, value)
+                elif name == "w1s":
+                    spread_parts(*chains[c][0:3])
+                elif name == "w2s":
+                    spread_parts(*chains[c][3:6])
                 elif name == "base":
                     prepare(c, step)
                 elif name == "y":
@@ -360,15 +369,19 @@
                     held[c, "e"] = back_dots(c)
                 elif name == "end":
                     back_end(c, *held[c, "e"])
-                elif name == "w2":
-                    update_second(c)
+                elif name in ("w2", "w2f"):
+                    refs, value = update_second(c)
+                    refs[0][...] = value
+                    if name == "w2f":
+                        store_parts(refs, value)
 
     for c in range(n_chains):
         w1f, w1hm, w1lo, w2f, w2hm, w2lo, b1r, b2r, zb, cor, dh8, hps, slope, d3r = chains[c]
-        store_first((w1f, w1hm, w1lo), w1[...])
+        w1f[...] = w1[...]
+        spread_parts(w1f, w1hm, w1lo)
         w2t = w2[...].T
-        w2t = w2t - jnp.mean(w2t, axis=0, keepdims=True)
-        store_first((w2f, w2hm, w2lo), w2t)
+        w2f[...] = w2t - jnp.mean(w2t, axis=0, keepdims=True)
+        spread_parts(w2f, w2hm, w2lo)
         b1r[...] = b_one[pl.ds(head, 1), :]
         b2 = b_two[pl.ds(head, 1), :]
         b2r[...] = b2 - jnp.mean(b2, axis=1, keepdims=True)
@@ -400,6 +413,10 @@
         send_some(2, (2, 1, 3, 0), step == (me - 1) * PACE)
         send_some(3, (2, 1, 3, 0), step == (me - half + 1) * PACE)
 
+        @pl.when(step == per_block)
+        def _():
+            pl.semaphore_wait(ready_sem, n_hp - 1)
+
         number = (step - 1) // per_piece - 1
         finished = (lax.rem(step, per_piece) == 1) & (step > per_piece)
 
@@ -423,7 +440,6 @@
         def _():
             for off in range(1, n_hp):
                 w_copy(off).wait_recv()
-            pl.semaphore_wait(ready_sem, n_hp - 1)
 
         @pl.when((since_group >= 0) & (since_group < first_direct * period) & (lax.rem(since_group, period) == 0))
         def _():
@@ -440,7 +456,7 @@
     def last_output(c):
         if c % 2 == 0:
             z = hidden_in(c)
-            update_second(c)
+            store_parts(*update_second(c))
             yield
             activate(c, z)
         yield
@@ -449,8 +465,9 @@
         xhat, _ = normalised(c, r, yl)
         store_out(c, n_steps - 1, load(c, 2, n_steps - 1).astype(F32) + gain * xhat[:MINI] + bias)
 
+    send_out(n_groups * n_sp - 1, True, pl.ds(0, PIECE - MINI))
     take_turns([last_output(c) for c in range(n_chains)])
-    send_out(n_groups * n_sp - 1, True)
+    send_out(n_groups * n_sp - 1, True, pl.ds(PIECE - MINI, MINI))
     for group in range(first_direct, n_groups):
         spread = gath.at[group, pl.ds(0, n_all - 1)]
         pltpu.make_async_copy(spread, spread, orecv_sem.at[group]).wait()

time: 100 us -> 96 us (0.960)
  the two profiles are of different devices: /device:TPU:103 before, /device:TPU:97 now
where the time goes in v4:
time: 96 us; the launch traced here: 95.9 us
  Pallas kernels  94 us (98%)
  local copies, waits for them, and re-layouts  1.87 us (2%)
    pallas_call x1, Pallas kernels, run(): pl.pallas_call(functools.partial(ttt_kernel, n_hp, n_sp, n_chains), out_s...  94 us

profile of v4, /device:TPU:97, one launch (start us, length us, event | category | flops | bytes accessed | tf_op | source)
XLA Modules:
  0.0 95.9 jit_solution(9357492006241660612)
XLA Ops:
  0.0 94.0 %shard_map.118 = bf16[4,128,512]{2,1,0:T(8,128)(2,1)} custom-call(bf16[4,128,2048]{2,1,0:T(8,128)(2,1)} %tokens.1, bf16[2048,512]{1,0:T(8,128)(2,1)} %theta_k.1, bf16[2048,512]{1,0:T(8,128)(2,1)} %theta_v.1, bf16[2048,512]{1,0:T(8,128)(2,1)} %theta_q.1, bf16[512,2048]{1,0:T(8,128)(2,1)} %w_out.1, f32[4,128,512]{2,1,0:T(8,128)} %w_one.1, ...), custom_call_target="tpu_custom_call" | custom-call | tf_op jit(solution)/shard_map/pallas_call | solution.py:534
  94.0 1.9 %copy.14 = bf16[4,128,512]{2,1,0:T(8,128)(2,1)} copy(bf16[4,128,512]{2,1,0:T(8,128)(2,1)} %shard_map.118) | data formatting | bytes 1048576
